TPU v7x, 32 devices: a whole 2x2x4 slice. The times are simulated.
32 devices in a mesh: dp: 8 (over z, y), mp: 4 (over x, core).
Axes of the slice: x: 2, y: 2, z: 4, core: 2. Of those that a mesh axis runs over, the one named last changes fastest.
Arguments:
- gradient: bfloat16 [8, 64, 14336], P('dp', None, 'mp'), may hold values from -6 to 6
- momentum: float32 [8, 64, 14336], P('dp', None, 'mp'), may hold values from -6 to 6
- weights: float32 [64, 14336], P(None, 'mp'), may hold values from -6 to 6
- positions: int32 [8, 1, 224, 32], P('dp', None, 'mp'), may hold values from 0 to 4095, as said below
Outputs:
- new_momentum: float32 [8, 64, 14336], P('dp', None, 'mp')
- new_weights: float32 [64, 14336], P(None, 'mp')
Inputs may be any that keep to these rules, and one draw needn't show every extreme that they name: Within one span of one replica the 32 positions are all different.
All inputs are finite; a program needn't handle non-finite values.
Results may differ from a plain program's by a relative error of at most 0.0003.
Values sent between devices are 32-bit elements; how exact they have to be, the bound alone decides.
No kernel may reach another device: no remote copies, remote signals or barrier semaphores. Data moves between devices by JAX's collectives and lax.ppermute only.
A program may use at most 64 MiB of HBM per device.

v0:
```python
import math

import jax
import jax.numpy as jnp
from jax import lax
from jax.sharding import PartitionSpec as P

FF = 14336


def dct_table():
    column = jnp.arange(64, dtype=jnp.float32)
    freq = column[:, None]
    factor = jnp.where(freq == 0, jnp.sqrt(jnp.float32(1.0 / 64)), jnp.sqrt(jnp.float32(2.0 / 64)))
    return factor * jnp.cos(jnp.pi * (2.0 * column[None, :] + 1.0) * freq / 128.0)


def paired_table(table):
    ident = jnp.eye(2, dtype=jnp.float32)
    return (ident[:, None, :, None] * table[None, :, None, :]).reshape(128, 128)


def forward_dct(field, table, paired):
    bands, height, width = field.shape
    along = jnp.einsum("kr,brf->bkf", table, field, precision=lax.Precision.HIGHEST)
    grouped = along.reshape(bands, height, width // 128, 128)
    result = jnp.einsum("bkgs,ls->bkgl", grouped, paired, precision=lax.Precision.HIGHEST)
    return result.reshape(bands, height, width)


def inverse_dct(coefs, table, paired):
    bands, height, width = coefs.shape
    grouped = coefs.reshape(bands, height, width // 128, 128)
    across = jnp.einsum("bkgl,ls->bkgs", grouped, paired, precision=lax.Precision.HIGHEST)
    across = across.reshape(bands, height, width)
    return jnp.einsum("kr,bkf->brf", table, across, precision=lax.Precision.HIGHEST)


def to_spans(field):
    bands, height, width = field.shape
    split = field.reshape(bands, 64, width // 64, 64)
    return jnp.transpose(split, (0, 2, 1, 3))


def from_spans(spans):
    bands, count, height, width = spans.shape
    return jnp.transpose(spans, (0, 2, 1, 3)).reshape(bands, 64, count * 64)


def decode_group(values, places):
    freqs = jnp.arange(64, dtype=jnp.int32)
    row_hot = (places[..., None] // 64 == freqs).astype(jnp.float32) * values[..., None]
    col_hot = (places[..., None] % 64 == freqs).astype(jnp.float32)
    return jnp.einsum("nbcjk,nbcjl->bckl", row_hot, col_hot, precision=lax.Precision.HIGHEST)


def decode_lists(values, places):
    count = values.shape[0]
    group = math.gcd(count, 8)
    steps = count // group
    if steps == 1:
        return decode_group(values, places)

    def add_group(index, total):
        part_values = lax.dynamic_slice_in_dim(values, index * group, group, 0)
        part_places = lax.dynamic_slice_in_dim(places, index * group, group, 0)
        return total + decode_group(part_values, part_places)

    start = jnp.zeros((values.shape[1], values.shape[2], 64, 64), jnp.float32)
    return lax.fori_loop(0, steps, add_group, start)


def local(gradient, momentum, weights, positions):
    table = dct_table()
    paired = paired_table(table)
    summed = 0.9 * momentum[0] + gradient[0].astype(jnp.float32)
    bands = summed.shape[0] // 64
    count = summed.shape[1] // 64
    coefs = forward_dct(summed.reshape(bands, 64, summed.shape[1]), table, paired)
    flattened = to_spans(coefs).reshape(bands, count, 4096)
    own_places = positions[0]
    picked = jnp.take_along_axis(flattened, own_places, axis=2)
    own = decode_group(picked[None], own_places[None])
    back = inverse_dct(from_spans(own), table, paired)
    new_momentum = (summed - back.reshape(summed.shape))[None]
    aggregate = decode_lists(
        lax.all_gather(picked[None], "dp", axis=0, tiled=True),
        lax.all_gather(own_places[None].astype(jnp.float32), "dp", axis=0, tiled=True).astype(
            jnp.int32
        ),
    )
    update = inverse_dct(from_spans(aggregate), table, paired).reshape(weights.shape)
    total_sq = lax.psum(jnp.sum(update * update), "mp")
    meansq = total_sq / (weights.shape[0] * FF)
    new_weights = weights - update / jnp.sqrt(meansq + 1.0)
    return (new_momentum, new_weights)


def solution(mesh):
    placed = (P("dp", None, "mp"), P("dp", None, "mp"), P(None, "mp"), P("dp", None, "mp", None))
    return jax.shard_map(
        local,
        mesh=mesh,
        in_specs=placed,
        out_specs=(P("dp", None, "mp"), P(None, "mp")),
        check_vma=False,
    )
```

profile of v0, /device:TPU:0, one launch (start us, length us, event | category | flops | bytes accessed | tf_op | source)
XLA Modules:
  0.0 132.9 jit_solution(11840959320905657482)
XLA Ops:
  0.6 0.0 copy-start
  0.6 0.0 copy-start.2
  0.7 0.8 fusion.34
  1.5 0.1 copy.34
  1.6 0.1 reshape.444
  1.7 0.7 convert_element_type.28
  2.4 0.8 copy.30
  3.2 0.1 cosine_multiply_fusion
  3.4 0.1 broadcast_multiply_fusion
  3.5 0.1 reshape.454
  3.6 32.3 %all_gather.6 = f32[8,1,56,32]{2,3,1,0:T(8,128)S(1)} all-gather(f32[1,1,56,32]{2,3,1,0:T(8,128)S(1)} %convert_element_type.28), channel_id=1, replica_groups=mesh['dp'=8,'mp'=4] {'dp'}, dimensions={0}, use_global_device_ids=true | all-gather | bytes 64512 | tf_op jit(solution)/shard_map/all_gather | solution.py:88
  35.9 0.1 add_select_fusion.1
  36.0 0.8 copy.38
  36.9 0.8 copy.44
  37.7 0.0 copy-done
  37.7 0.0 copy-done.2
  37.7 1.2 convolution_bitcast_fusion.1
  38.9 0.2 reshape.436
  39.1 1.5 %fusion.18 = f32[64,28,128]{2,0,1:T(8,128)S(1)} fusion(f32[128,128,1]{1,0,2:T(8,128)S(1)} %reshape.454, f32[64,28,128]{2,1,0:T(8,128)S(1)} %reshape.436), kind=kOutput, calls=%fused_computation.25 | convolution fusion | flops 352321536 | bytes 1900544 | tf_op jit(solution)/shard_map/bkgs,ls->bkgl/dot_general | solution.py:27
  40.5 0.5 copy.32
  41.1 0.3 reshape_reshape.2
  41.4 1.6 %copy.33 = f32[1,56,64,64]{3,2,1,0:T(8,128)} copy(f32[1,56,64,64]{3,1,2,0:T(8,128)S(1)} %bitcast.113) | data formatting | bytes 1835008 | tf_op jit(solution)/shard_map/transpose | solution.py:42
  43.0 2.1 %reshape.442 = f32[56,4096]{1,0:T(8,128)S(1)} reshape(f32[1,56,64,64]{3,2,1,0:T(8,128)} %copy.33) | data formatting | bytes 1835008 | tf_op jit(solution)/shard_map/reshape | solution.py:80
  45.1 0.0 copy-start.4
  45.1 0.0 copy-start.5
  45.1 14.0 %gather_fusion = f32[1792]{0:T(1024)S(1)} fusion(f32[56,4096]{1,0:T(8,128)S(1)} %reshape.442, s32[1792]{0:T(1024)S(1)} %reshape.444), kind=kCustom, calls=%fused_computation | custom fusion | bytes 28672 | tf_op jit(solution)/shard_map/jit(take_along_axis)/gather | solution.py:82
  59.1 0.1 gather.9
  59.1 0.1 gather.10
  59.2 0.1 copy.42
  59.3 30.5 %all_gather.7 = f32[8,1,56,32]{2,3,1,0:T(8,128)S(1)} all-gather(f32[1,1,56,32]{2,3,1,0:T(8,128)S(1)} %copy.42), channel_id=1, replica_groups=mesh['dp'=8,'mp'=4] {'dp'}, dimensions={0}, use_global_device_ids=true | all-gather | bytes 64512 | tf_op jit(solution)/shard_map/all_gather | solution.py:87
  89.8 0.1 copy.43
  90.0 0.0 copy-done.4
  90.0 0.0 copy-done.5
  90.0 22.1 %fusion.7 = f32[1,64,56,64]{3,1,2,0:T(8,128)S(1)} fusion(s32[8,56,32]{2,0,1:T(8,128)S(1)} %copy-done.5, f32[8,56,32]{2,0,1:T(8,128)S(1)} %copy.43, s32[8,56,32]{2,0,1:T(8,128)S(1)} %copy-done.4), kind=kOutput, calls=%fused_computation.13 | convolution fusion | flops 707395584 | bytes 1089536 | tf_op jit(solution)/shard_map/nbcjk,nbcjl->bckl/dot_general | solution.py:54
  112.1 1.1 copy.45
  113.1 0.3 reshape.440
  113.5 1.5 %convolution_bitcast_fusion.3 = f32[28,8,8,128]{3,2,1,0:T(8,128)S(1)} fusion(f32[128,128,1]{1,0,2:T(8,128)S(1)} %reshape.454, f32[64,28,128]{2,1,0:T(8,128)S(1)} %reshape.440), kind=kOutput, calls=%fused_computation.14 | convolution fusion | flops 352321536 | bytes 1900544 | tf_op jit(solution)/shard_map/bkgl,ls->bkgs/dot_general | solution.py:34
  114.9 0.0 copy-start.3
  114.9 1.8 %multiply_reduce_fusion = (f32[]{:T(128)}, f32[3584,64]{0,1:T(8,128)S(1)}) fusion(f32[64]{0:T(128)S(1)} %get-tuple-element.9, f32[64]{0:T(128)S(1)} %get-tuple-element.8, f32[28,8,8,128]{3,2,1,0:T(8,128)S(1)} %convolution_bitcast_fusion.3), kind=kOutput, calls=%fused_computation.27 | convolution fusion | flops 176631808 | bytes 1835524 | tf_op jit(solution)/shard_map/kr,bkf->brf/dot_general | solution.py:36
  116.7 6.4 %psum.7 = f32[]{:T(128)} all-reduce(f32[]{:T(128)} %get-tuple-element.6), channel_id=1, replica_groups=mesh['dp'=8,'mp'=4] {'mp'}, use_global_device_ids=true, to_apply=%region_1.2 | all-reduce | flops 1 | bytes 8 | tf_op jit(solution)/shard_map/psum | solution.py:93
  123.8 0.0 copy-done.3
  123.9 1.0 bitcast_subtract_fusion
  124.9 3.1 %convolution_bitcast_fusion.2 = f32[1,64,56,64]{3,1,2,0:T(8,128)S(1)} fusion(s32[56,32]{1,0:T(8,128)S(1)} %get-tuple-element.5, f32[56,32]{1,0:T(8,128)S(1)} %and_select_fusion.1, s32[56,32]{1,0:T(8,128)S(1)} %get-tuple-element.4), kind=kOutput, calls=%fused_computation.12 | convolution fusion | flops 88424448 | bytes 939008 | tf_op jit(solution)/shard_map/nbcjk,nbcjl->bckl/dot_general | solution.py:54
  127.9 1.1 copy.35
  129.0 0.3 reshape.438
  129.3 0.0 copy-start.1
  129.3 1.5 %convolution_bitcast_fusion.4 = f32[28,8,8,128]{3,2,1,0:T(8,128)S(1)} fusion(f32[128,128,1]{1,0,2:T(8,128)S(1)} %reshape.454, f32[64,28,128]{2,1,0:T(8,128)S(1)} %reshape.438), kind=kOutput, calls=%fused_computation.15 | convolution fusion | flops 352321536 | bytes 1900544 | tf_op jit(solution)/shard_map/bkgl,ls->bkgs/dot_general | solution.py:34
  130.8 0.0 copy-done.1
  130.8 2.0 %fusion.2 = f32[1,64,3584]{2,1,0:T(8,128)} fusion(f32[28,8,8,128]{3,2,1,0:T(8,128)S(1)} %convolution_bitcast_fusion.4, bf16[1,64,3584]{2,1,0:T(8,128)(2,1)S(1)} %copy-done.2, f32[1,64,3584]{2,1,0:T(8,128)S(1)} %copy-done.1, f32[64]{0:T(128)S(1)} %get-tuple-element.9, f32[64]{0:T(128)S(1)} %get-tuple-element.8), kind=kOutput, calls=%fused_computation.7 | convolution fusion | flops 177090560 | bytes 3211776 | tf_op jit(solution)/shard_map/kr,bkf->brf/dot_general | solution.py:36
  (5 shorter events, 0.1 us)
Async XLA Ops:
  0.6 37.0 %copy-start = (f32[1,64,3584]{2,1,0:T(8,128)S(1)}, f32[1,64,3584]{2,1,0:T(8,128)}, u32[]{:S(2)}) copy-start(f32[1,64,3584]{2,1,0:T(8,128)} %param.5) | copy-start | bytes 2752516
  0.6 37.0 %copy-start.2 = (bf16[1,64,3584]{2,1,0:T(8,128)(2,1)S(1)}, bf16[1,64,3584]{2,1,0:T(8,128)(2,1)}, u32[]{:S(2)}) copy-start(bf16[1,64,3584]{2,1,0:T(8,128)(2,1)} %param.4) | copy-start | bytes 1376260
  45.1 44.9 %copy-start.4 = (s32[8,56,32]{2,0,1:T(8,128)S(1)}, s32[8,56,32]{2,0,1:T(8,128)}, u32[]{:S(2)}) copy-start(s32[8,56,32]{2,0,1:T(8,128)} %copy.38) | copy-start | bytes 172036
  45.1 44.9 %copy-start.5 = (s32[8,56,32]{2,0,1:T(8,128)S(1)}, s32[8,56,32]{2,0,1:T(8,128)}, u32[]{:S(2)}) copy-start(s32[8,56,32]{2,0,1:T(8,128)} %copy.44) | copy-start | bytes 172036
  114.9 8.9 %copy-start.3 = (f32[64,3584]{1,0:T(8,128)S(1)}, f32[64,3584]{1,0:T(8,128)}, u32[]{:S(2)}) copy-start(f32[64,3584]{1,0:T(8,128)} %param.6) | copy-start | bytes 2752516
  129.3 1.5 %copy-start.1 = (f32[1,64,3584]{2,1,0:T(8,128)S(1)}, f32[1,64,3584]{2,1,0:T(8,128)}, u32[]{:S(2)}) copy-start(f32[1,64,3584]{2,1,0:T(8,128)} %param.5) | copy-start | bytes 2752516
where the time goes:
time: 133 us
  blocking collectives  69.3 us (52%)
  matrix products  34.5 us (26%)
  local copies, waits for them, and re-layouts  24.5 us (18%)
  other arithmetic  3.01 us (2%)
  between operations  1.57 us (1%)
    all_gather x1, blocking collectives, local(): lax.all_gather(own_places[None].astype(jnp.float32), 'dp', axis=0, tiled=...  32.3 us
    all_gather x1, blocking collectives, local(): lax.all_gather(picked[None], 'dp', axis=0, tiled=True)  30.5 us
    dot_general x2, matrix products, decode_group(): jnp.einsum('nbcjk,nbcjl->bckl', row_hot, col_hot, precision=lax.Precision...  25.1 us
    gather x5, local copies, waits for them, and re-layouts, local(): picked = jnp.take_along_axis(flattened, own_places, axis=2)  14.3 us
    psum x1, blocking collectives, local(): total_sq = lax.psum(jnp.sum(update * update), 'mp')  6.45 us
    dot_general x2, matrix products, inverse_dct(): jnp.einsum('kr,bkf->brf', table, across, precision=lax.Precision.HIGHEST)  3.8 us
    dot_general x2, matrix products, inverse_dct(): jnp.einsum('bkgl,ls->bkgs', grouped, paired, precision=lax.Precision.HIGH...  2.93 us

commit v1 on v0

v1 whole, which is shorter than its diff:
```python
import functools

import jax
import jax.numpy as jnp
import numpy as np
from jax import lax
from jax.experimental import pallas as pl
from jax.experimental.pallas import tpu as pltpu
from jax.sharding import PartitionSpec as P

SPAN = 64
QUAD = 4
WIDE = SPAN * QUAD
F32 = jnp.float32
BF16 = jnp.bfloat16


def dct_table():
    column = np.arange(SPAN, dtype=np.float64)
    factor = np.where(column == 0, np.sqrt(1.0 / SPAN), np.sqrt(2.0 / SPAN))
    angle = np.pi * (2.0 * column[None, :] + 1.0) * column[:, None] / (2.0 * SPAN)
    return (factor[:, None] * np.cos(angle)).astype(np.float32)


def halves(table):
    high = table.astype(BF16)
    return high, (table - high.astype(np.float32)).astype(BF16)


def row_operand(table):
    high, low = halves(table)
    return np.concatenate([high, high, low], axis=1)


def lane_operand(table):
    return halves(np.kron(np.eye(QUAD, dtype=np.float32), table))


def split(value):
    high = value.astype(BF16)
    return high, (value - high.astype(F32)).astype(BF16)


def dot(left, right):
    return lax.dot_general(left, right, (((1,), (0,)), ((), ())), preferred_element_type=F32)


def dot_t(left, right):
    return lax.dot_general(left, right, (((1,), (1,)), ((), ())), preferred_element_type=F32)


def along_rows(operand, field):
    high, low = split(field)
    return dot(operand, jnp.concatenate([high, low, high], axis=0))


def along_lanes(field, high_table, low_table):
    high, low = split(field)
    return dot(high, high_table) + dot(low, high_table) + dot(high, low_table)


def lane_target(place):
    quarter = lax.broadcasted_iota(jnp.int32, place.shape, 1) // (128 // QUAD)
    return quarter * SPAN + place % SPAN


def hot(size, wanted):
    grid = lax.broadcasted_iota(jnp.int32, (size, wanted.shape[1]), 0)
    return grid == wanted


def pick_kernel(grad, mom, place, rows, high, low, message, coefs):
    groups = place.shape[0]
    message[...] = jnp.zeros_like(message)
    message[0, 16 : 16 + groups, :] = place[...].astype(F32)
    row_of = place[...] // SPAN
    lane_of = lane_target(place[...])
    for index in range(groups):
        lanes = slice(index * WIDE, (index + 1) * WIDE)
        summed = 0.9 * mom[0, :, lanes] + grad[0, :, lanes].astype(F32)
        along = along_rows(rows[...], summed)
        coef = along_lanes(along, high[...], low[...])
        coefs[:, lanes] = coef
        lane_hot = hot(WIDE, lane_of[index : index + 1]).astype(F32).astype(BF16)
        coef_high, coef_low = split(coef)
        columns = dot(coef_high, lane_hot) + dot(coef_low, lane_hot)
        chosen = jnp.where(hot(SPAN, row_of[index : index + 1]), columns, 0.0)
        message[0, index : index + 1, :] = jnp.sum(chosen, axis=0, keepdims=True)


def momentum_kernel(grad, mom, place, coefs, rows, high, low, out):
    groups = place.shape[0]
    row_of = place[...] // SPAN
    lane_of = lane_target(place[...])
    for index in range(groups):
        lanes = slice(index * WIDE, (index + 1) * WIDE)
        row_hot = hot(SPAN, row_of[index : index + 1]).astype(F32).astype(BF16)
        lane_hot = hot(WIDE, lane_of[index : index + 1]).astype(F32).astype(BF16)
        own = coefs[:, lanes] * dot_t(row_hot, lane_hot)
        across = along_lanes(own, high[...], low[...])
        back = along_rows(rows[...], across)
        summed = 0.9 * mom[0, :, lanes] + grad[0, :, lanes].astype(F32)
        out[0, :, lanes] = summed - back


def decode_group(index, order, lists, count):
    total = jnp.zeros((SPAN, WIDE), F32)
    for step in range(count):
        which = step ^ order
        value = lists[which, index : index + 1, :]
        place = lists[which, 16 + index : 17 + index, :].astype(jnp.int32)
        high = value.astype(BF16).astype(F32)
        row_hot = hot(SPAN, place // SPAN)
        lane_hot = hot(WIDE, lane_target(place)).astype(F32).astype(BF16)
        left = jnp.where(row_hot, high, 0.0).astype(BF16)
        right = jnp.where(row_hot, value - high, 0.0).astype(BF16)
        total = total + (dot_t(left, lane_hot) + dot_t(right, lane_hot))
    return total


def decode_kernel(groups, order, lists, out):
    low = order[0]
    for index in range(groups):
        lanes = slice(index * WIDE, (index + 1) * WIDE)
        out[:, lanes] = decode_group(index, low, lists, lists.shape[0])


def decode_last_kernel(groups, order, lists, held, out, squares):
    low = order[0]
    squared = jnp.zeros((8, WIDE), F32)
    for index in range(groups):
        lanes = slice(index * WIDE, (index + 1) * WIDE)
        total = held[:, lanes] + decode_group(index, low, lists, lists.shape[0])
        out[:, lanes] = total
        squared = squared + jnp.sum((total * total).reshape(8, 8, WIDE), axis=0)
    squares[...] = squared[:, :128] + squared[:, 128:]


def update_kernel(total, rows, high, low, out):
    for index in range(total.shape[1] // WIDE):
        lanes = slice(index * WIDE, (index + 1) * WIDE)
        out[:, lanes] = along_rows(rows[...], along_lanes(total[:, lanes], high[...], low[...]))


def apply_kernel(entries, weights, update, squares, out):
    scale = lax.rsqrt(jnp.sum(squares[...]) / entries + 1.0)
    out[...] = weights[...] - update[...] * scale


def call(kernel, shapes, flops, *args, smem=()):
    specs = [
        pl.BlockSpec(memory_space=pltpu.SMEM if at in smem else pltpu.VMEM)
        for at in range(len(args))
    ]
    out_specs = jax.tree.map(lambda _: pl.BlockSpec(memory_space=pltpu.VMEM), shapes)
    return pl.pallas_call(
        kernel,
        out_shape=shapes,
        in_specs=specs,
        out_specs=out_specs,
        cost_estimate=pl.CostEstimate(flops=flops, bytes_accessed=4 * SPAN * 3584, transcendentals=0),
        compiler_params=pltpu.CompilerParams(vmem_limit_bytes=24 * 1024 * 1024),
    )(*args)


def local(replicas, parts, gradient, momentum, weights, positions):
    table = dct_table()
    forward = row_operand(table), *lane_operand(table.T)
    inverse = row_operand(table.T), *lane_operand(table)
    forward = [jnp.asarray(part) for part in forward]
    inverse = [jnp.asarray(part) for part in inverse]
    height, width = weights.shape
    groups = width // WIDE
    place = positions.reshape(groups, 128)
    field = jax.ShapeDtypeStruct((height, width), F32)
    message, coefs = call(
        pick_kernel,
        (jax.ShapeDtypeStruct((1, 32, 128), F32), field),
        1 << 30,
        gradient,
        momentum,
        place,
        *forward,
    )
    new_momentum = call(
        momentum_kernel,
        jax.ShapeDtypeStruct(momentum.shape, F32),
        1 << 31,
        gradient,
        momentum,
        place,
        coefs,
        *inverse,
    )
    held = message
    bit = 1
    while 2 * bit < replicas:
        other = lax.ppermute(held, "dp", [(at, at ^ bit) for at in range(replicas)])
        held = jnp.concatenate([held, other], axis=0)
        bit *= 2
    order = (lax.axis_index("dp") % bit).reshape(1)
    other = lax.ppermute(held, "dp", [(at, at ^ bit) for at in range(replicas)])
    own_total = call(
        functools.partial(decode_kernel, groups), field, 1 << 30, order, held, smem=(0,)
    )
    total, squares = call(
        functools.partial(decode_last_kernel, groups),
        (field, jax.ShapeDtypeStruct((8, 128), F32)),
        1 << 30,
        order,
        other,
        own_total,
        smem=(0,),
    )
    update = call(update_kernel, field, 1 << 31, total, *inverse)
    step = 1
    while step < parts:
        squares = squares + lax.ppermute(squares, "mp", [(at, at ^ step) for at in range(parts)])
        step *= 2
    new_weights = call(
        functools.partial(apply_kernel, float(height * width * parts)),
        field,
        1 << 20,
        weights,
        update,
        squares,
    )
    return new_momentum, new_weights


def solution(mesh):
    placed = (P("dp", None, "mp"), P("dp", None, "mp"), P(None, "mp"), P("dp", None, "mp", None))
    return jax.shard_map(
        functools.partial(local, mesh.shape["dp"], mesh.shape["mp"]),
        mesh=mesh,
        in_specs=placed,
        out_specs=(P("dp", None, "mp"), P(None, "mp")),
        check_vma=False,
    )
```

time: 133 us -> 41.4 us (0.31)
  blocking collectives: 69.3 us -> 0 us
  matrix products: 34.5 us -> 0 us
  Pallas kernels: 0 us -> 22 us
  local copies, waits for them, and re-layouts: 24.5 us -> 4.94 us
  starting transfers between devices: 0 us -> 9.73 us
  waiting for transfers between devices: 0 us -> 3.61 us
  other arithmetic: 3.01 us -> 0.01 us
    all_gather x2 -> x0, blocking collectives: 62.8 us -> none  [the longest x1 32.3 us: local(): lax.all_gather(own_places[None].astype(jnp.float32), 'dp', axis=0, tiled=...]
    dot_general x8 -> x0, matrix products: 34.5 us -> none  [the longest x2 25.1 us: decode_group(): jnp.einsum('nbcjk,nbcjl->bckl', row_hot, col_hot, precision=lax.Precision...]
    pallas_call x0 -> x6, Pallas kernels: none -> 22 us  [call(): pl.pallas_call(kernel, out_shape=shapes, in_specs=specs, out_specs=out_sp...]
    gather x5 -> x0, local copies, waits for them, and re-layouts: 14.3 us -> none  [local(): picked = jnp.take_along_axis(flattened, own_places, axis=2)]
    ppermute x0 -> x5, starting transfers between devices: none -> 9.73 us  [the longest x3 8.17 us: local(): other = lax.ppermute(held, 'dp', [(at, at ^ bit) for at in range(replicas)])]
    psum x1 -> x0, blocking collectives: 6.45 us -> none  [local(): total_sq = lax.psum(jnp.sum(update * update), 'mp')]
    unnamed x13 -> x25, local copies, waits for them, and re-layouts: 0.83 us -> 4.86 us
    transpose x3 -> x0, local copies, waits for them, and re-layouts: 3.72 us -> none  [the longest x2 2.13 us: from_spans(): return jnp.transpose(spans, (0, 2, 1, 3)).reshape(bands, 64, count * 64)]
  transfers between devices with their start and end apart: 0 -> 5, of which waited for: 0 -> 2; matrix products, arithmetic and copies ran while one was open for 0% -> 0% of each run, Pallas kernels for 0% -> 31%
where the time goes in v1:
time: 41.4 us; the launch traced here: 41.1 us
  Pallas kernels  22 us (53%)
  starting transfers between devices  9.73 us (24%)
  local copies, waits for them, and re-layouts  4.94 us (12%)
  waiting for transfers between devices  3.61 us (9%)
  between operations  0.79 us (2%)
    pallas_call x6, Pallas kernels, call(): pl.pallas_call(kernel, out_shape=shapes, in_specs=specs, out_specs=out_sp...  22 us
    ppermute x3, starting transfers between devices, local(): other = lax.ppermute(held, 'dp', [(at, at ^ bit) for at in range(replicas)])  8.17 us
    unnamed x25, local copies, waits for them, and re-layouts  4.86 us
    ppermute x3, waiting for transfers between devices, local(): other = lax.ppermute(held, 'dp', [(at, at ^ bit) for at in range(replicas)])  3.61 us
    ppermute x2, starting transfers between devices, local(): lax.ppermute(squares, 'mp', [(at, at ^ step) for at in range(parts)])  1.56 us
  transfers between devices with their start and end apart: 5, of which 2 were waited for; matrix products, arithmetic and copies ran while one was open for 0% of the time, Pallas kernels for 31%

profile of v1, /device:TPU:0, one launch (start us, length us, event | category | flops | bytes accessed | tf_op | source)
XLA Modules:
  0.0 41.1 jit_solution(4481519653282515221)
XLA Ops:
  0.6 0.0 copy-start.10
  0.6 0.8 %copy.13 = s32[1,1,56,32]{3,2,1,0:T(8,128)S(1)} copy(s32[1,1,56,32]{2,3,1,0:T(8,128)} %param.13) | data formatting | bytes 14336 | tf_op args[3]
  1.4 0.1 reshape.10.place
  1.5 0.0 copy-done.10
  1.5 0.0 copy-start.1
  1.5 1.2 %copy-done.1 = f32[1,64,3584]{2,1,0:T(8,128)S(1)} copy-done((f32[1,64,3584]{2,1,0:T(8,128)S(1)}, f32[1,64,3584]{2,1,0:T(8,128)}, u32[]{:S(2)}) %copy-start.1) | copy-done | bytes 917528
  2.7 0.0 copy-start.3
  2.7 1.0 %copy-done.3 = bf16[1,64,3584]{2,1,0:T(8,128)(2,1)S(1)} copy-done((bf16[1,64,3584]{2,1,0:T(8,128)(2,1)S(1)}, bf16[1,64,3584]{2,1,0:T(8,128)(2,1)}, u32[]{:S(2)}) %copy-start.3) | copy-done | bytes 458776
  3.7 0.0 copy-start.7
  3.7 0.9 %copy-done.7 = bf16[256,256]{1,0:T(8,128)(2,1)S(1)} copy-done((bf16[256,256]{1,0:T(8,128)(2,1)S(1)}, bf16[256,256]{1,0:T(8,128)(2,1)}, u32[]{:S(2)}) %copy-start.7) | copy-done | bytes 131096
  4.6 0.0 copy-start.8
  4.6 0.9 %copy-done.8 = bf16[256,256]{1,0:T(8,128)(2,1)S(1)} copy-done((bf16[256,256]{1,0:T(8,128)(2,1)S(1)}, bf16[256,256]{1,0:T(8,128)(2,1)}, u32[]{:S(2)}) %copy-start.8) | copy-done | bytes 131096
  5.5 5.2 %shard_map.113 = (f32[1,32,128]{2,1,0:T(8,128)S(1)}, f32[64,3584]{1,0:T(8,128)S(1)}) custom-call(bf16[1,64,3584]{2,1,0:T(8,128)(2,1)S(1)} %copy-done.3, f32[1,64,3584]{2,1,0:T(8,128)S(1)} %copy-done.1, s32[14,128]{1,0:T(8,128)S(1)} %reshape.10.place, bf16[64,192]{1,0:T(8,128)(2,1)S(1)} %copy-done.10, bf16[256,256]{1,0:T(8,128)(2,1)S(1)} %copy-done.8, ...), custom_call_target="tpu_custom_call" | custom-call | flops 1073741824 | bytes 917504 | tf_op jit(solution)/shard_map/pallas_call | solution.py:156
  10.7 3.1 %collective-permute-start = (f32[1,32,128]{2,1,0:T(8,128)S(1)}, f32[1,32,128]{2,1,0:T(8,128)S(1)}, u32[]{:S(2)}, u32[]{:S(2)}) collective-permute-start(f32[1,32,128]{2,1,0:T(8,128)S(1)} %get-tuple-element.7), channel_id=1, source_target_pairs={{0,4},{4,0},{8,12},{12,8},{16,20},{20,16},{24,28},{28,24},{1,5},{5... | collective-permute-start | bytes 49160 | tf_op jit(solution)/shard_map/ppermute | solution.py:198
  13.8 1.7 %collective-permute-done = f32[1,32,128]{2,1,0:T(8,128)S(1)} collective-permute-done((f32[1,32,128]{2,1,0:T(8,128)S(1)}, f32[1,32,128]{2,1,0:T(8,128)S(1)}, u32[]{:S(2)}, u32[]{:S(2)}) %collective-permute-start) | collective-permute-done | bytes 16416 | tf_op jit(solution)/shard_map/ppermute | solution.py:198
  15.5 2.1 %collective-permute-start.1 = (f32[2,32,128]{2,1,0:T(8,128)S(1)}, f32[2,32,128]{2,1,0:T(8,128)S(1)}, u32[]{:S(2)}, u32[]{:S(2)}) collective-permute-start(f32[2,32,128]{2,1,0:T(8,128)S(1)} %pad_maximum_fusion), channel_id=1, source_target_pairs={{0,8},{4,12},{8,0},{12,4},{16,24},{20,28},{24,16},{28,20},{1,9},{5... | collective-permute-start | bytes 98312 | tf_op jit(solution)/shard_map/ppermute | solution.py:198
  17.6 1.9 %collective-permute-done.1 = f32[2,32,128]{2,1,0:T(8,128)S(1)} collective-permute-done((f32[2,32,128]{2,1,0:T(8,128)S(1)}, f32[2,32,128]{2,1,0:T(8,128)S(1)}, u32[]{:S(2)}, u32[]{:S(2)}) %collective-permute-start.1) | collective-permute-done | bytes 32800 | tf_op jit(solution)/shard_map/ppermute | solution.py:198
  19.5 3.0 %collective-permute-start.2 = (f32[4,32,128]{2,1,0:T(8,128)S(1)}, f32[4,32,128]{2,1,0:T(8,128)S(1)}, u32[]{:S(2)}, u32[]{:S(2)}) collective-permute-start(f32[4,32,128]{2,1,0:T(8,128)S(1)} %constant_dynamic-update-slice_fusion.lists), channel_id=1, source_target_pairs={{0,16},{4,20},{8,24},{12,28},{16,0},{20,4},{24,8},{28,12},{1,17},{... | collective-permute-start | bytes 196616 | tf_op jit(solution)/shard_map/ppermute | solution.py:202
  22.5 2.7 %shard_map.115.held = f32[64,3584]{1,0:T(8,128)S(1)} custom-call(s32[1]{0:T(128)} %bitcast.order, f32[4,32,128]{2,1,0:T(8,128)S(1)} %constant_dynamic-update-slice_fusion.lists), custom_call_target="tpu_custom_call" | custom-call | flops 1073741824 | bytes 917504 | tf_op jit(solution)/shard_map/pallas_call | solution.py:156
  25.2 0.0 copy-start.2
  25.3 0.0 copy-start.4
  25.3 0.0 copy-start.5
  25.3 0.0 copy-start.6
  25.3 0.0 copy-start.9
  25.3 0.0 collective-permute-done.2.lists
  25.3 2.8 %shard_map.116 = (f32[64,3584]{1,0:T(8,128)S(1)}, f32[8,128]{1,0:T(8,128)S(1)}) custom-call(s32[1]{0:T(128)} %bitcast.order, f32[4,32,128]{2,1,0:T(8,128)S(1)} %collective-permute-done.2.lists, f32[64,3584]{1,0:T(8,128)S(1)} %shard_map.115.held), custom_call_target="tpu_custom_call" | custom-call | flops 1073741824 | bytes 917504 | tf_op jit(solution)/shard_map/pallas_call | solution.py:156
  28.1 0.1 collective-permute-start.3
  28.1 0.0 copy-done.2
  28.2 0.0 copy-done.4
  28.2 0.0 copy-done.5
  28.2 0.0 copy-done.6
  28.2 0.0 copy-done.9
  28.2 6.4 %shard_map.114 = f32[1,64,3584]{2,1,0:T(8,128)} custom-call(bf16[1,64,3584]{2,1,0:T(8,128)(2,1)S(1)} %copy-done.4, f32[1,64,3584]{2,1,0:T(8,128)S(1)} %copy-done.2, s32[14,128]{1,0:T(8,128)S(1)} %reshape.10.place, f32[64,3584]{1,0:T(8,128)S(1)} %get-tuple-element.6.coefs, bf16[64,192]{1,0:T(8,128)(2,1)S(1)} %copy-done.9, bf16[256,256]{1,0:T(8,128)(2,1)S(1)} %copy-done.6, ...), custom_call_target="tpu_custom_call" | custom-call | flops 2147483648 | bytes 917504 | tf_op jit(solution)/shard_map/pallas_call | solution.py:156
  34.6 0.0 collective-permute-done.3
  34.6 1.5 %collective-permute-start.4 = (f32[8,128]{1,0:T(8,128)S(1)}, f32[8,128]{1,0:T(8,128)S(1)}, u32[]{:S(2)}, u32[]{:S(2)}) collective-permute-start(f32[8,128]{1,0:T(8,128)S(1)} %add.11), channel_id=1, source_target_pairs={{0,2},{1,3},{2,0},{3,1},{4,6},{5,7},{6,4},{7,5},{8,10},{9,11},{10,... | collective-permute-start | bytes 12296 | tf_op jit(solution)/shard_map/ppermute | solution.py:218
  36.1 0.0 copy-start
  36.1 3.8 %shard_map.117.update = f32[64,3584]{1,0:T(8,128)S(1)} custom-call(f32[64,3584]{1,0:T(8,128)S(1)} %get-tuple-element.8.total, bf16[64,192]{1,0:T(8,128)(2,1)S(1)} %copy-done.9, bf16[256,256]{1,0:T(8,128)(2,1)S(1)} %copy-done.6, bf16[256,256]{1,0:T(8,128)(2,1)S(1)} %copy-done.5), custom_call_target="tpu_custom_call" | custom-call | flops 2147483648 | bytes 917504 | tf_op jit(solution)/shard_map/pallas_call | solution.py:156
  39.8 0.0 collective-permute-done.4
  39.9 0.0 copy-done
  39.9 1.2 %shard_map.118 = f32[64,3584]{1,0:T(8,128)} custom-call(f32[64,3584]{1,0:T(8,128)S(1)} %copy-done, f32[64,3584]{1,0:T(8,128)S(1)} %shard_map.117.update, f32[8,128]{1,0:T(8,128)S(1)} %add.12.squares), custom_call_target="tpu_custom_call" | custom-call | flops 1048576 | bytes 917504 | tf_op jit(solution)/shard_map/pallas_call | solution.py:156
  (6 shorter events, 0.0 us)
Async XLA Ops:
  0.6 0.9 %copy-start.10 = (bf16[64,192]{1,0:T(8,128)(2,1)S(1)}, bf16[64,192]{1,0:T(8,128)(2,1)}, u32[]{:S(2)}) copy-start(bf16[64,192]{1,0:T(8,128)(2,1)} %constant.31.clone.rows) | copy-start | bytes 73732
  1.5 1.2 %copy-start.1 = (f32[1,64,3584]{2,1,0:T(8,128)S(1)}, f32[1,64,3584]{2,1,0:T(8,128)}, u32[]{:S(2)}) copy-start(f32[1,64,3584]{2,1,0:T(8,128)} %mom.3) | copy-start | bytes 2752516
  2.7 1.0 %copy-start.3 = (bf16[1,64,3584]{2,1,0:T(8,128)(2,1)S(1)}, bf16[1,64,3584]{2,1,0:T(8,128)(2,1)}, u32[]{:S(2)}) copy-start(bf16[1,64,3584]{2,1,0:T(8,128)(2,1)} %grad.3) | copy-start | bytes 1376260
  3.7 0.9 %copy-start.7 = (bf16[256,256]{1,0:T(8,128)(2,1)S(1)}, bf16[256,256]{1,0:T(8,128)(2,1)}, u32[]{:S(2)}) copy-start(bf16[256,256]{1,0:T(8,128)(2,1)} %constant.33.clone.low) | copy-start | bytes 393220
  4.6 0.9 %copy-start.8 = (bf16[256,256]{1,0:T(8,128)(2,1)S(1)}, bf16[256,256]{1,0:T(8,128)(2,1)}, u32[]{:S(2)}) copy-start(bf16[256,256]{1,0:T(8,128)(2,1)} %constant.32.clone.high) | copy-start | bytes 393220
  10.7 4.8 %collective-permute-start = (f32[1,32,128]{2,1,0:T(8,128)S(1)}, f32[1,32,128]{2,1,0:T(8,128)S(1)}, u32[]{:S(2)}, u32[]{:S(2)}) collective-permute-start(f32[1,32,128]{2,1,0:T(8,128)S(1)} %get-tuple-element.7), channel_id=1, source_target_pairs={{0,4},{4,0},{8,12},{12,8},{16,20},{20,16},{24,28},{28,24},{1,5},{5... | collective-permute-start | bytes 49160 | tf_op jit(solution)/shard_map/ppermute | solution.py:198
  15.5 4.0 %collective-permute-start.1 = (f32[2,32,128]{2,1,0:T(8,128)S(1)}, f32[2,32,128]{2,1,0:T(8,128)S(1)}, u32[]{:S(2)}, u32[]{:S(2)}) collective-permute-start(f32[2,32,128]{2,1,0:T(8,128)S(1)} %pad_maximum_fusion), channel_id=1, source_target_pairs={{0,8},{4,12},{8,0},{12,4},{16,24},{20,28},{24,16},{28,20},{1,9},{5... | collective-permute-start | bytes 98312 | tf_op jit(solution)/shard_map/ppermute | solution.py:198
  19.5 5.8 %collective-permute-start.2 = (f32[4,32,128]{2,1,0:T(8,128)S(1)}, f32[4,32,128]{2,1,0:T(8,128)S(1)}, u32[]{:S(2)}, u32[]{:S(2)}) collective-permute-start(f32[4,32,128]{2,1,0:T(8,128)S(1)} %constant_dynamic-update-slice_fusion.lists), channel_id=1, source_target_pairs={{0,16},{4,20},{8,24},{12,28},{16,0},{20,4},{24,8},{28,12},{1,17},{... | collective-permute-start | bytes 196616 | tf_op jit(solution)/shard_map/ppermute | solution.py:202
  25.2 2.9 %copy-start.2 = (f32[1,64,3584]{2,1,0:T(8,128)S(1)}, f32[1,64,3584]{2,1,0:T(8,128)}, u32[]{:S(2)}) copy-start(f32[1,64,3584]{2,1,0:T(8,128)} %mom.3) | copy-start | bytes 2752516
  25.3 2.9 %copy-start.4 = (bf16[1,64,3584]{2,1,0:T(8,128)(2,1)S(1)}, bf16[1,64,3584]{2,1,0:T(8,128)(2,1)}, u32[]{:S(2)}) copy-start(bf16[1,64,3584]{2,1,0:T(8,128)(2,1)} %grad.3) | copy-start | bytes 1376260
  25.3 2.9 %copy-start.5 = (bf16[256,256]{1,0:T(8,128)(2,1)S(1)}, bf16[256,256]{1,0:T(8,128)(2,1)}, u32[]{:S(2)}) copy-start(bf16[256,256]{1,0:T(8,128)(2,1)} %constant.36.clone.low) | copy-start | bytes 393220
  25.3 2.9 %copy-start.6 = (bf16[256,256]{1,0:T(8,128)(2,1)S(1)}, bf16[256,256]{1,0:T(8,128)(2,1)}, u32[]{:S(2)}) copy-start(bf16[256,256]{1,0:T(8,128)(2,1)} %constant.35.clone.high) | copy-start | bytes 393220
  25.3 2.9 %copy-start.9 = (bf16[64,192]{1,0:T(8,128)(2,1)S(1)}, bf16[64,192]{1,0:T(8,128)(2,1)}, u32[]{:S(2)}) copy-start(bf16[64,192]{1,0:T(8,128)(2,1)} %constant.34.clone.rows) | copy-start | bytes 73732
  28.1 6.5 %collective-permute-start.3 = (f32[8,128]{1,0:T(8,128)S(1)}, f32[8,128]{1,0:T(8,128)S(1)}, u32[]{:S(2)}, u32[]{:S(2)}) collective-permute-start(f32[8,128]{1,0:T(8,128)S(1)} %get-tuple-element.9), channel_id=1, source_target_pairs={{0,1},{1,0},{2,3},{3,2},{4,5},{5,4},{6,7},{7,6},{8,9},{9,8},{10,11... | collective-permute-start | bytes 12296 | tf_op jit(solution)/shard_map/ppermute | solution.py:218
  34.6 5.3 %collective-permute-start.4 = (f32[8,128]{1,0:T(8,128)S(1)}, f32[8,128]{1,0:T(8,128)S(1)}, u32[]{:S(2)}, u32[]{:S(2)}) collective-permute-start(f32[8,128]{1,0:T(8,128)S(1)} %add.11), channel_id=1, source_target_pairs={{0,2},{1,3},{2,0},{3,1},{4,6},{5,7},{6,4},{7,5},{8,10},{9,11},{10,... | collective-permute-start | bytes 12296 | tf_op jit(solution)/shard_map/ppermute | solution.py:218
  36.1 3.8 %copy-start = (f32[64,3584]{1,0:T(8,128)S(1)}, f32[64,3584]{1,0:T(8,128)}, u32[]{:S(2)}) copy-start(f32[64,3584]{1,0:T(8,128)} %weights.1) | copy-start | bytes 2752516

commit v2 on v1

v2 whole, which is shorter than its diff:
```python
import functools

import jax
import jax.numpy as jnp
import numpy as np
from jax import lax
from jax.experimental import pallas as pl
from jax.experimental.pallas import tpu as pltpu
from jax.sharding import PartitionSpec as P

SPAN = 64
QUAD = 4
WIDE = SPAN * QUAD
F32 = jnp.float32
BF16 = jnp.bfloat16
VMEM_LIMIT = 24 * 1024 * 1024


def dct_table():
    column = np.arange(SPAN, dtype=np.float64)
    factor = np.where(column == 0, np.sqrt(1.0 / SPAN), np.sqrt(2.0 / SPAN))
    angle = np.pi * (2.0 * column[None, :] + 1.0) * column[:, None] / (2.0 * SPAN)
    return (factor[:, None] * np.cos(angle)).astype(np.float32)


def halves(table):
    high = table.astype(BF16)
    return high, (table - high.astype(np.float32)).astype(BF16)


def operands(table):
    high, low = halves(table)
    rows = np.concatenate([high, high, low, np.zeros_like(low)], axis=1)
    blocks = halves(np.kron(np.eye(QUAD, dtype=np.float32), table.T))
    return np.concatenate([rows, *blocks], axis=0)


def split(value):
    high = value.astype(BF16)
    return high, (value - high.astype(F32)).astype(BF16)


def dot(left, right):
    return lax.dot_general(left, right, (((1,), (0,)), ((), ())), preferred_element_type=F32)


def dot_t(left, right):
    return lax.dot_general(left, right, (((1,), (1,)), ((), ())), preferred_element_type=F32)


def row_table(tables):
    return tables[:SPAN, : 3 * SPAN]


def along_lanes(high, low, tables):
    high_table = tables[SPAN : SPAN + WIDE, :]
    low_table = tables[SPAN + WIDE :, :]
    return dot(high, high_table) + dot(low, high_table) + dot(high, low_table)


def put_rows(stack, lanes, value):
    high, low = split(value)
    stack[:SPAN, lanes] = high
    stack[SPAN : 2 * SPAN, lanes] = low
    stack[2 * SPAN :, lanes] = high


def lane_target(place):
    quarter = lax.broadcasted_iota(jnp.int32, place.shape, 1) // (128 // QUAD)
    return quarter * SPAN + place % SPAN


def counter(size):
    return lax.broadcasted_iota(jnp.int32, (size, 128), 0).astype(F32).astype(BF16).reshape(size // 16, 16, 128)


def same(count, wanted):
    row = jnp.broadcast_to(wanted, (16, wanted.shape[1])).astype(BF16)
    return count == row[None]


def ones_at(count, wanted):
    mask = same(count, wanted)
    return jnp.where(mask, jnp.ones((), BF16), jnp.zeros((), BF16)).reshape(-1, 128)


def value_at(count, wanted, value):
    row = jnp.broadcast_to(value, (16, 128)).astype(BF16)
    mask = same(count, wanted)
    return jnp.where(mask, jnp.broadcast_to(row[None], count.shape), jnp.zeros((), BF16)).reshape(-1, 128)


def pick_kernel(chunks, grad, mom, place, table, message, coefs, summed, g_buf, m_buf, p_buf, t_buf, turned, stack, high, low, lane_hot, sems):
    width = summed.shape[1]
    groups = width // WIDE
    step = width // chunks

    copies = [
        pltpu.make_async_copy(place, p_buf, sems.at[2 * chunks]),
        pltpu.make_async_copy(table, t_buf, sems.at[2 * chunks + 1]),
    ]
    for at in range(chunks):
        lanes = pl.ds(at * step, step)
        copies.append(pltpu.make_async_copy(grad.at[0, :, lanes], g_buf.at[:, lanes], sems.at[2 * at]))
        copies.append(pltpu.make_async_copy(mom.at[0, :, lanes], m_buf.at[:, lanes], sems.at[2 * at + 1]))
    for copy in copies:
        copy.start()
    copies[0].wait()
    turned[...] = jnp.transpose(p_buf[...])
    places = jnp.concatenate([turned[pl.ds(at, groups, stride=QUAD), :] for at in range(QUAD)], axis=1)
    message[...] = jnp.zeros_like(message)
    message[0, 16 : 16 + groups, :] = places.astype(F32)
    row_of = (places // SPAN).astype(F32)
    lane_of = lane_target(places).astype(F32)
    wide = counter(WIDE)
    for index in range(groups):
        lane_hot[index] = ones_at(wide, lane_of[index : index + 1])
    for at in range(chunks):
        lanes = slice(at * step, (at + 1) * step)
        copies[2 + 2 * at].wait()
        copies[3 + 2 * at].wait()
        total = 0.9 * m_buf[:, lanes] + g_buf[:, lanes].astype(F32)
        summed[:, lanes] = total
        put_rows(stack, lanes, total)
    copies[1].wait()
    along = dot(row_table(t_buf), stack[...])
    for index in range(groups):
        rows = slice(index * SPAN, (index + 1) * SPAN)
        high[rows, :], low[rows, :] = split(along[:, index * WIDE : (index + 1) * WIDE])
    coefs[...] = along_lanes(high[...], low[...], t_buf)
    grid = lax.broadcasted_iota(jnp.int32, (SPAN, 128), 0).astype(F32)
    for index in range(groups):
        coef_high, coef_low = split(coefs[index * SPAN : (index + 1) * SPAN, :])
        columns = dot(jnp.concatenate([coef_high, coef_low], axis=0), lane_hot[index])
        columns = columns[:SPAN] + columns[SPAN:]
        chosen = jnp.where(grid == row_of[index : index + 1], columns, 0.0)
        message[0, index : index + 1, :] = jnp.sum(chosen, axis=0, keepdims=True)


def inverse(high, low, tables, stack, groups):
    across = along_lanes(high[...], low[...], tables)
    for index in range(groups):
        lanes = slice(index * WIDE, (index + 1) * WIDE)
        put_rows(stack, lanes, across[index * SPAN : (index + 1) * SPAN, :])
    return dot(row_table(tables), stack[...])


def momentum_kernel(summed, message, coefs, tables, out, high, low, stack):
    groups = summed.shape[1] // WIDE
    places = message[0, 16 : 16 + groups, :].astype(jnp.int32)
    row_of = (places // SPAN).astype(F32)
    lane_of = lane_target(places).astype(F32)
    narrow, wide = counter(SPAN), counter(WIDE)
    for index in range(groups):
        rows = slice(index * SPAN, (index + 1) * SPAN)
        row_hot = ones_at(narrow, row_of[index : index + 1])
        lane_hot = ones_at(wide, lane_of[index : index + 1])
        own = coefs[rows, :] * dot_t(row_hot, lane_hot)
        high[rows, :], low[rows, :] = split(own)
    out[0] = summed[...] - inverse(high, low, tables, stack, groups)


def prepare(order, lists, groups, value_of, row_of, lane_of):
    for step in range(lists.shape[0]):
        which = step ^ order
        value_of[step] = lists[which, :groups, :]
        places = lists[which, 16 : 16 + groups, :].astype(jnp.int32)
        row_of[step] = (places // SPAN).astype(F32)
        lane_of[step] = lane_target(places).astype(F32)


def decode_group(index, narrow, wide, value_of, row_of, lane_of):
    left, right = [], []
    for step in range(value_of.shape[0]):
        value = value_of[step, index : index + 1, :]
        wanted = row_of[step, index : index + 1, :]
        high = value.astype(BF16).astype(F32)
        left.append(
            jnp.concatenate([value_at(narrow, wanted, high), value_at(narrow, wanted, value - high)], axis=0)
        )
        right.append(ones_at(wide, lane_of[step, index : index + 1, :]))
    total = dot_t(jnp.concatenate(left, axis=1), jnp.concatenate(right, axis=1))
    return total[:SPAN] + total[SPAN:]


def decode_kernel(groups, order, lists, out, value_of, row_of, lane_of):
    prepare(order[0], lists, groups, value_of, row_of, lane_of)
    narrow, wide = counter(SPAN), counter(WIDE)
    for index in range(groups):
        out[index * SPAN : (index + 1) * SPAN, :] = decode_group(index, narrow, wide, value_of, row_of, lane_of)


def decode_last_kernel(groups, order, lists, held, out, squares, value_of, row_of, lane_of):
    prepare(order[0], lists, groups, value_of, row_of, lane_of)
    narrow, wide = counter(SPAN), counter(WIDE)
    squared = jnp.zeros((8, WIDE), F32)
    for index in range(groups):
        rows = slice(index * SPAN, (index + 1) * SPAN)
        total = held[rows, :] + decode_group(index, narrow, wide, value_of, row_of, lane_of)
        out[rows, :] = total
        squared = squared + jnp.sum((total * total).reshape(8, 8, WIDE), axis=0)
    squares[...] = squared[:, :128] + squared[:, 128:]


def update_kernel(total, tables, out, high, low, stack):
    groups = total.shape[0] // SPAN
    for index in range(groups):
        rows = slice(index * SPAN, (index + 1) * SPAN)
        high[rows, :], low[rows, :] = split(total[rows, :])
    out[...] = inverse(high, low, tables, stack, groups)


def apply_kernel(entries, weights, update, squares, out):
    scale = lax.rsqrt(jnp.sum(squares[...]) / entries + 1.0)
    out[...] = weights[...] - update[...] * scale


def call(kernel, shapes, flops, *args, spaces=None, scratch=()):
    spaces = spaces or {}
    specs = [pl.BlockSpec(memory_space=spaces.get(at, pltpu.VMEM)) for at in range(len(args))]
    out_specs = jax.tree.map(lambda _: pl.BlockSpec(memory_space=pltpu.VMEM), shapes)
    return pl.pallas_call(
        kernel,
        out_shape=shapes,
        in_specs=specs,
        out_specs=out_specs,
        scratch_shapes=list(scratch),
        cost_estimate=pl.CostEstimate(flops=flops, bytes_accessed=1 << 20, transcendentals=0),
        compiler_params=pltpu.CompilerParams(vmem_limit_bytes=VMEM_LIMIT),
    )(*args)


def local(replicas, parts, gradient, momentum, weights, positions):
    table = dct_table()
    forward = jnp.asarray(operands(table))
    backward = jnp.asarray(operands(table.T))
    height, width = weights.shape
    groups = width // WIDE
    spans, kept = positions.shape[2:]
    chunks = 7
    field = jax.ShapeDtypeStruct((height, width), F32)
    tall = jax.ShapeDtypeStruct((groups * SPAN, WIDE), F32)
    half = pltpu.VMEM((groups * SPAN, WIDE), BF16)
    stack = pltpu.VMEM((3 * SPAN, width), BF16)
    message, coefs, summed = call(
        functools.partial(pick_kernel, chunks),
        (jax.ShapeDtypeStruct((1, 32, 128), F32), tall, field),
        1 << 30,
        pltpu.with_memory_space_constraint(gradient, pltpu.HBM),
        pltpu.with_memory_space_constraint(momentum, pltpu.HBM),
        pltpu.with_memory_space_constraint(jnp.swapaxes(positions[0, 0], 0, 1), pltpu.HBM),
        pltpu.with_memory_space_constraint(forward, pltpu.HBM),
        spaces={0: pltpu.HBM, 1: pltpu.HBM, 2: pltpu.HBM, 3: pltpu.HBM},
        scratch=(
            pltpu.VMEM((height, width), BF16),
            pltpu.VMEM((height, width), F32),
            pltpu.VMEM((kept, spans), jnp.int32),
            pltpu.VMEM(forward.shape, BF16),
            pltpu.VMEM((spans, kept), jnp.int32),
            stack,
            half,
            half,
            pltpu.VMEM((groups, WIDE, 128), BF16),
            pltpu.SemaphoreType.DMA((2 * chunks + 2,)),
        ),
    )
    new_momentum = call(
        momentum_kernel,
        jax.ShapeDtypeStruct(momentum.shape, F32),
        1 << 31,
        summed,
        message,
        coefs,
        backward,
        scratch=(half, half, stack),
    )
    held = message
    bit = 1
    while 2 * bit < replicas:
        other = lax.ppermute(held, "dp", [(at, at ^ bit) for at in range(replicas)])
        held = jnp.concatenate([held, other], axis=0)
        bit *= 2
    order = (lax.axis_index("dp") % bit).reshape(1)
    other = lax.ppermute(held, "dp", [(at, at ^ bit) for at in range(replicas)])
    tables = tuple(pltpu.VMEM((bit, groups, 128), F32) for _ in range(3))
    own_total = call(
        functools.partial(decode_kernel, groups),
        tall,
        1 << 30,
        order,
        held,
        spaces={0: pltpu.SMEM},
        scratch=tables,
    )
    total, squares = call(
        functools.partial(decode_last_kernel, groups),
        (tall, jax.ShapeDtypeStruct((8, 128), F32)),
        1 << 30,
        order,
        other,
        own_total,
        spaces={0: pltpu.SMEM},
        scratch=tables,
    )
    update = call(update_kernel, field, 1 << 31, total, backward, scratch=(half, half, stack))
    step = 1
    while step < parts:
        squares = squares + lax.ppermute(squares, "mp", [(at, at ^ step) for at in range(parts)])
        step *= 2
    new_weights = call(
        functools.partial(apply_kernel, float(height * width * parts)),
        field,
        1 << 20,
        weights,
        update,
        squares,
    )
    return new_momentum, new_weights


def solution(mesh):
    placed = (P("dp", None, "mp"), P("dp", None, "mp"), P(None, "mp"), P("dp", None, "mp", None))
    return jax.shard_map(
        functools.partial(local, mesh.shape["dp"], mesh.shape["mp"]),
        mesh=mesh,
        in_specs=placed,
        out_specs=(P("dp", None, "mp"), P(None, "mp")),
        check_vma=False,
    )
```

time: 41.4 us -> 26.4 us (0.64)
  Pallas kernels: 22 us -> 10.1 us
  local copies, waits for them, and re-layouts: 4.94 us -> 0.02 us
  waiting for transfers between devices: 3.61 us -> 5.32 us
    pallas_call x6, Pallas kernels: 22 us -> 10.1 us  [call(): pl.pallas_call(kernel, out_shape=shapes, in_specs=specs, out_specs=out_sp...]
    unnamed x25 -> x6, local copies, waits for them, and re-layouts: 4.86 us -> 0.01 us
    ppermute x3, waiting for transfers between devices: 3.61 us -> 4.49 us  [local(): other = lax.ppermute(held, 'dp', [(at, at ^ bit) for at in range(replicas)])]
    ppermute x2, waiting for transfers between devices: 0.01 us -> 0.84 us  [local(): lax.ppermute(squares, 'mp', [(at, at ^ step) for at in range(parts)])]
  transfers between devices with their start and end apart: 5 -> 5, of which waited for: 2 -> 4; matrix products, arithmetic and copies ran while one was open for 0% -> 0% of each run, Pallas kernels for 31% -> 17%
where the time goes in v2:
time: 26.4 us; the launch traced here: 26.2 us
  Pallas kernels  10.1 us (38%)
  starting transfers between devices  10.1 us (38%)
  waiting for transfers between devices  5.32 us (20%)
  between operations  0.69 us (3%)
    pallas_call x6, Pallas kernels, call(): pl.pallas_call(kernel, out_shape=shapes, in_specs=specs, out_specs=out_sp...  10.1 us
    ppermute x3, starting transfers between devices, local(): other = lax.ppermute(held, 'dp', [(at, at ^ bit) for at in range(replicas)])  8.17 us
    ppermute x3, waiting for transfers between devices, local(): other = lax.ppermute(held, 'dp', [(at, at ^ bit) for at in range(replicas)])  4.49 us
    ppermute x2, starting transfers between devices, local(): lax.ppermute(squares, 'mp', [(at, at ^ step) for at in range(parts)])  1.9 us
    ppermute x2, waiting for transfers between devices, local(): lax.ppermute(squares, 'mp', [(at, at ^ step) for at in range(parts)])  0.84 us
  transfers between devices with their start and end apart: 5, of which 4 were waited for; matrix products, arithmetic and copies ran while one was open for 0% of the time, Pallas kernels for 17%

profile of v2, /device:TPU:0, one launch (start us, length us, event | category | flops | bytes accessed | tf_op | source)
XLA Modules:
  0.0 26.2 jit_solution(11067395680545410880)
XLA Ops:
  0.6 3.0 %shard_map.77 = (f32[1,32,128]{2,1,0:T(8,128)S(1)}, f32[896,256]{1,0:T(8,128)S(1)}, f32[64,3584]{1,0:T(8,128)S(1)}) custom-call(bf16[1,64,3584]{2,1,0:T(8,128)(2,1)} %grad.1, f32[1,64,3584]{2,1,0:T(8,128)} %mom.1, s32[32,56]{1,0:T(8,128)} %bitcast.4, bf16[576,256]{1,0:T(8,128)(2,1)} %constant.23.clone.table), custom_call_target="tpu_custom_call" | custom-call | flops 1073741824 | bytes 1048576 | tf_op jit(solution)/shard_map/pallas_call | solution.py:222
  3.6 3.1 %collective-permute-start = (f32[1,32,128]{2,1,0:T(8,128)S(1)}, f32[1,32,128]{2,1,0:T(8,128)S(1)}, u32[]{:S(2)}, u32[]{:S(2)}) collective-permute-start(f32[1,32,128]{2,1,0:T(8,128)S(1)} %get-tuple-element.8.message), channel_id=1, source_target_pairs={{0,4},{4,0},{8,12},{12,8},{16,20},{20,16},{24,28},{28,24},{1,5},{5... | collective-permute-start | bytes 49160 | tf_op jit(solution)/shard_map/ppermute | solution.py:280
  6.7 1.7 %collective-permute-done = f32[1,32,128]{2,1,0:T(8,128)S(1)} collective-permute-done((f32[1,32,128]{2,1,0:T(8,128)S(1)}, f32[1,32,128]{2,1,0:T(8,128)S(1)}, u32[]{:S(2)}, u32[]{:S(2)}) %collective-permute-start) | collective-permute-done | bytes 16416 | tf_op jit(solution)/shard_map/ppermute | solution.py:280
  8.4 2.1 %collective-permute-start.1 = (f32[2,32,128]{2,1,0:T(8,128)S(1)}, f32[2,32,128]{2,1,0:T(8,128)S(1)}, u32[]{:S(2)}, u32[]{:S(2)}) collective-permute-start(f32[2,32,128]{2,1,0:T(8,128)S(1)} %pad_maximum_fusion), channel_id=1, source_target_pairs={{0,8},{4,12},{8,0},{12,4},{16,24},{20,28},{24,16},{28,20},{1,9},{5... | collective-permute-start | bytes 98312 | tf_op jit(solution)/shard_map/ppermute | solution.py:280
  10.5 1.9 %collective-permute-done.1 = f32[2,32,128]{2,1,0:T(8,128)S(1)} collective-permute-done((f32[2,32,128]{2,1,0:T(8,128)S(1)}, f32[2,32,128]{2,1,0:T(8,128)S(1)}, u32[]{:S(2)}, u32[]{:S(2)}) %collective-permute-start.1) | collective-permute-done | bytes 32800 | tf_op jit(solution)/shard_map/ppermute | solution.py:280
  12.4 3.0 %collective-permute-start.2 = (f32[4,32,128]{2,1,0:T(8,128)S(1)}, f32[4,32,128]{2,1,0:T(8,128)S(1)}, u32[]{:S(2)}, u32[]{:S(2)}) collective-permute-start(f32[4,32,128]{2,1,0:T(8,128)S(1)} %constant_dynamic-update-slice_fusion.lists), channel_id=1, source_target_pairs={{0,16},{4,20},{8,24},{12,28},{16,0},{20,4},{24,8},{28,12},{1,17},{... | collective-permute-start | bytes 196616 | tf_op jit(solution)/shard_map/ppermute | solution.py:284
  15.4 1.3 %shard_map.79.held = f32[896,256]{1,0:T(8,128)S(1)} custom-call(s32[1]{0:T(128)} %bitcast.2.order, f32[4,32,128]{2,1,0:T(8,128)S(1)} %constant_dynamic-update-slice_fusion.lists), custom_call_target="tpu_custom_call" | custom-call | flops 1073741824 | bytes 1048576 | tf_op jit(solution)/shard_map/pallas_call | solution.py:222
  16.8 0.0 copy-start.1
  16.8 0.9 %collective-permute-done.2.lists = f32[4,32,128]{2,1,0:T(8,128)S(1)} collective-permute-done((f32[4,32,128]{2,1,0:T(8,128)S(1)}, f32[4,32,128]{2,1,0:T(8,128)S(1)}, u32[]{:S(2)}, u32[]{:S(2)}) %collective-permute-start.2) | collective-permute-done | bytes 65568 | tf_op jit(solution)/shard_map/ppermute | solution.py:284
  17.7 1.4 %shard_map.80 = (f32[896,256]{1,0:T(8,128)S(1)}, f32[8,128]{1,0:T(8,128)S(1)}) custom-call(s32[1]{0:T(128)} %bitcast.2.order, f32[4,32,128]{2,1,0:T(8,128)S(1)} %collective-permute-done.2.lists, f32[896,256]{1,0:T(8,128)S(1)} %shard_map.79.held), custom_call_target="tpu_custom_call" | custom-call | flops 1073741824 | bytes 1048576 | tf_op jit(solution)/shard_map/pallas_call | solution.py:222
  19.0 0.1 collective-permute-start.3
  19.1 0.0 copy-done.1
  19.1 2.2 %shard_map.78 = f32[1,64,3584]{2,1,0:T(8,128)} custom-call(f32[64,3584]{1,0:T(8,128)S(1)} %get-tuple-element.7.summed, f32[1,32,128]{2,1,0:T(8,128)S(1)} %get-tuple-element.8.message, f32[896,256]{1,0:T(8,128)S(1)} %get-tuple-element.9.coefs, bf16[576,256]{1,0:T(8,128)(2,1)S(1)} %copy-done.1), custom_call_target="tpu_custom_call" | custom-call | flops 2147483648 | bytes 1048576 | tf_op jit(solution)/shard_map/pallas_call | solution.py:222
  21.3 0.0 collective-permute-done.3
  21.3 1.8 %collective-permute-start.4 = (f32[8,128]{1,0:T(8,128)S(1)}, f32[8,128]{1,0:T(8,128)S(1)}, u32[]{:S(2)}, u32[]{:S(2)}) collective-permute-start(f32[8,128]{1,0:T(8,128)S(1)} %add.11), channel_id=1, source_target_pairs={{0,2},{1,3},{2,0},{3,1},{4,6},{5,7},{6,4},{7,5},{8,10},{9,11},{10,... | collective-permute-start | bytes 12296 | tf_op jit(solution)/shard_map/ppermute | solution.py:308
  23.2 0.0 copy-start
  23.2 0.9 %shard_map.81.update = f32[64,3584]{1,0:T(8,128)S(1)} custom-call(f32[896,256]{1,0:T(8,128)S(1)} %get-tuple-element.10.total, bf16[576,256]{1,0:T(8,128)(2,1)S(1)} %copy-done.1), custom_call_target="tpu_custom_call" | custom-call | flops 2147483648 | bytes 1048576 | tf_op jit(solution)/shard_map/pallas_call | solution.py:222
  24.1 0.8 %collective-permute-done.4 = f32[8,128]{1,0:T(8,128)S(1)} collective-permute-done((f32[8,128]{1,0:T(8,128)S(1)}, f32[8,128]{1,0:T(8,128)S(1)}, u32[]{:S(2)}, u32[]{:S(2)}) %collective-permute-start.4) | collective-permute-done | bytes 4128 | tf_op jit(solution)/shard_map/ppermute | solution.py:308
  25.0 0.0 copy-done
  25.0 1.2 %shard_map.82 = f32[64,3584]{1,0:T(8,128)} custom-call(f32[64,3584]{1,0:T(8,128)S(1)} %copy-done, f32[64,3584]{1,0:T(8,128)S(1)} %shard_map.81.update, f32[8,128]{1,0:T(8,128)S(1)} %add.12.squares), custom_call_target="tpu_custom_call" | custom-call | flops 1048576 | bytes 1048576 | tf_op jit(solution)/shard_map/pallas_call | solution.py:222
  (6 shorter events, 0.0 us)
Async XLA Ops:
  3.6 4.8 %collective-permute-start = (f32[1,32,128]{2,1,0:T(8,128)S(1)}, f32[1,32,128]{2,1,0:T(8,128)S(1)}, u32[]{:S(2)}, u32[]{:S(2)}) collective-permute-start(f32[1,32,128]{2,1,0:T(8,128)S(1)} %get-tuple-element.8.message), channel_id=1, source_target_pairs={{0,4},{4,0},{8,12},{12,8},{16,20},{20,16},{24,28},{28,24},{1,5},{5... | collective-permute-start | bytes 49160 | tf_op jit(solution)/shard_map/ppermute | solution.py:280
  8.4 4.0 %collective-permute-start.1 = (f32[2,32,128]{2,1,0:T(8,128)S(1)}, f32[2,32,128]{2,1,0:T(8,128)S(1)}, u32[]{:S(2)}, u32[]{:S(2)}) collective-permute-start(f32[2,32,128]{2,1,0:T(8,128)S(1)} %pad_maximum_fusion), channel_id=1, source_target_pairs={{0,8},{4,12},{8,0},{12,4},{16,24},{20,28},{24,16},{28,20},{1,9},{5... | collective-permute-start | bytes 98312 | tf_op jit(solution)/shard_map/ppermute | solution.py:280
  12.4 5.3 %collective-permute-start.2 = (f32[4,32,128]{2,1,0:T(8,128)S(1)}, f32[4,32,128]{2,1,0:T(8,128)S(1)}, u32[]{:S(2)}, u32[]{:S(2)}) collective-permute-start(f32[4,32,128]{2,1,0:T(8,128)S(1)} %constant_dynamic-update-slice_fusion.lists), channel_id=1, source_target_pairs={{0,16},{4,20},{8,24},{12,28},{16,0},{20,4},{24,8},{28,12},{1,17},{... | collective-permute-start | bytes 196616 | tf_op jit(solution)/shard_map/ppermute | solution.py:284
  16.8 2.3 %copy-start.1 = (bf16[576,256]{1,0:T(8,128)(2,1)S(1)}, bf16[576,256]{1,0:T(8,128)(2,1)}, u32[]{:S(2)}) copy-start(bf16[576,256]{1,0:T(8,128)(2,1)} %constant.24.clone.tables) | copy-start | bytes 884740
  19.0 2.3 %collective-permute-start.3 = (f32[8,128]{1,0:T(8,128)S(1)}, f32[8,128]{1,0:T(8,128)S(1)}, u32[]{:S(2)}, u32[]{:S(2)}) collective-permute-start(f32[8,128]{1,0:T(8,128)S(1)} %get-tuple-element.11), channel_id=1, source_target_pairs={{0,1},{1,0},{2,3},{3,2},{4,5},{5,4},{6,7},{7,6},{8,9},{9,8},{10,11... | collective-permute-start | bytes 12296 | tf_op jit(solution)/shard_map/ppermute | solution.py:308
  21.3 3.6 %collective-permute-start.4 = (f32[8,128]{1,0:T(8,128)S(1)}, f32[8,128]{1,0:T(8,128)S(1)}, u32[]{:S(2)}, u32[]{:S(2)}) collective-permute-start(f32[8,128]{1,0:T(8,128)S(1)} %add.11), channel_id=1, source_target_pairs={{0,2},{1,3},{2,0},{3,1},{4,6},{5,7},{6,4},{7,5},{8,10},{9,11},{10,... | collective-permute-start | bytes 12296 | tf_op jit(solution)/shard_map/ppermute | solution.py:308
  23.2 1.8 %copy-start = (f32[64,3584]{1,0:T(8,128)S(1)}, f32[64,3584]{1,0:T(8,128)}, u32[]{:S(2)}) copy-start(f32[64,3584]{1,0:T(8,128)} %weights.1) | copy-start | bytes 2752516

commit v3 on v2

--- a/solution.py
+++ b/solution.py
@@ -90,11 +90,10 @@
     return jnp.where(mask, jnp.broadcast_to(row[None], count.shape), jnp.zeros((), BF16)).reshape(-1, 128)
 
 
-def pick_kernel(chunks, grad, mom, place, table, message, coefs, summed, g_buf, m_buf, p_buf, t_buf, turned, stack, high, low, lane_hot, sems):
+def pick_kernel(chunks, grad, mom, place, table, message, summed, sides, column, g_buf, m_buf, p_buf, t_buf, turned, hots, sems):
     width = summed.shape[1]
     groups = width // WIDE
     step = width // chunks
-
     copies = [
         pltpu.make_async_copy(place, p_buf, sems.at[2 * chunks]),
         pltpu.make_async_copy(table, t_buf, sems.at[2 * chunks + 1]),
@@ -105,36 +104,42 @@
         copies.append(pltpu.make_async_copy(mom.at[0, :, lanes], m_buf.at[:, lanes], sems.at[2 * at + 1]))
     for copy in copies:
         copy.start()
+    narrow = counter(SPAN)
+    lane = lax.broadcasted_iota(jnp.int32, (16, 128), 1) // (128 // QUAD)
+    masks = [jnp.where(lane == at, 1.0, 0.0).astype(BF16) == jnp.ones((), BF16) for at in range(QUAD)]
+    message[...] = jnp.zeros_like(message)
     copies[0].wait()
     turned[...] = jnp.transpose(p_buf[...])
     places = jnp.concatenate([turned[pl.ds(at, groups, stride=QUAD), :] for at in range(QUAD)], axis=1)
-    message[...] = jnp.zeros_like(message)
     message[0, 16 : 16 + groups, :] = places.astype(F32)
     row_of = (places // SPAN).astype(F32)
-    lane_of = lane_target(places).astype(F32)
-    wide = counter(WIDE)
-    for index in range(groups):
-        lane_hot[index] = ones_at(wide, lane_of[index : index + 1])
+    column_of = (places % SPAN).astype(F32)
+    for index in range(groups):
+        hots[:, index * WIDE : index * WIDE + 128] = ones_at(narrow, column_of[index : index + 1])
+        hots[:, index * WIDE + 128 : (index + 1) * WIDE] = ones_at(narrow, row_of[index : index + 1])
+    copies[1].wait()
+    chosen = dot(t_buf[...], hots[...])
+    for index in range(groups):
+        at = index * WIDE
+        for half in range(2):
+            tall = slice(half * SPAN, (half + 1) * SPAN)
+            piece = chosen[tall, at : at + 128].astype(BF16).reshape(SPAN // 16, 16, 128)
+            for quarter in range(QUAD):
+                kept = jnp.where(masks[quarter][None], piece, jnp.zeros((), BF16)).reshape(SPAN, 128)
+                sides[index, half, quarter * SPAN : (quarter + 1) * SPAN, :] = kept
+        column[index] = chosen[:SPAN, at + 128 : at + WIDE] + chosen[SPAN:, at + 128 : at + WIDE]
     for at in range(chunks):
         lanes = slice(at * step, (at + 1) * step)
         copies[2 + 2 * at].wait()
         copies[3 + 2 * at].wait()
         total = 0.9 * m_buf[:, lanes] + g_buf[:, lanes].astype(F32)
         summed[:, lanes] = total
-        put_rows(stack, lanes, total)
-    copies[1].wait()
-    along = dot(row_table(t_buf), stack[...])
-    for index in range(groups):
-        rows = slice(index * SPAN, (index + 1) * SPAN)
-        high[rows, :], low[rows, :] = split(along[:, index * WIDE : (index + 1) * WIDE])
-    coefs[...] = along_lanes(high[...], low[...], t_buf)
-    grid = lax.broadcasted_iota(jnp.int32, (SPAN, 128), 0).astype(F32)
-    for index in range(groups):
-        coef_high, coef_low = split(coefs[index * SPAN : (index + 1) * SPAN, :])
-        columns = dot(jnp.concatenate([coef_high, coef_low], axis=0), lane_hot[index])
-        columns = columns[:SPAN] + columns[SPAN:]
-        chosen = jnp.where(grid == row_of[index : index + 1], columns, 0.0)
-        message[0, index : index + 1, :] = jnp.sum(chosen, axis=0, keepdims=True)
+        for index in range(at * step // WIDE, (at + 1) * step // WIDE):
+            inner = index * WIDE - at * step
+            high, low = split(total[:, inner : inner + WIDE])
+            both = dot(jnp.concatenate([high, low], axis=0), sides[index, 0])
+            values = both[:SPAN] + both[SPAN:] + dot(high, sides[index, 1])
+            message[0, index : index + 1, :] = jnp.sum(values * column[index], axis=0, keepdims=True)
 
 
 def inverse(high, low, tables, stack, groups):
@@ -145,54 +150,62 @@
     return dot(row_table(tables), stack[...])
 
 
-def momentum_kernel(summed, message, coefs, tables, out, high, low, stack):
-    groups = summed.shape[1] // WIDE
-    places = message[0, 16 : 16 + groups, :].astype(jnp.int32)
-    row_of = (places // SPAN).astype(F32)
-    lane_of = lane_target(places).astype(F32)
-    narrow, wide = counter(SPAN), counter(WIDE)
-    for index in range(groups):
-        rows = slice(index * SPAN, (index + 1) * SPAN)
-        row_hot = ones_at(narrow, row_of[index : index + 1])
-        lane_hot = ones_at(wide, lane_of[index : index + 1])
-        own = coefs[rows, :] * dot_t(row_hot, lane_hot)
-        high[rows, :], low[rows, :] = split(own)
-    out[0] = summed[...] - inverse(high, low, tables, stack, groups)
+def momentum_kernel(message, summed, sides, column, out, buf, sems):
+    groups = column.shape[0]
+    copies = []
+    for index in range(groups):
+        lanes = pl.ds(index * WIDE, WIDE)
+        high, low = split(column[index] * message[0, index : index + 1, :])
+        both = dot_t(jnp.concatenate([high, low], axis=0), sides[index, 0])
+        buf[:, lanes] = summed[:, lanes] - (both[:SPAN] + both[SPAN:] + dot_t(high, sides[index, 1]))
+        copies.append(pltpu.make_async_copy(buf.at[:, lanes], out.at[0, :, lanes], sems.at[index]))
+        copies[-1].start()
+    for copy in copies:
+        copy.wait()
 
 
 def prepare(order, lists, groups, value_of, row_of, lane_of):
-    for step in range(lists.shape[0]):
-        which = step ^ order
-        value_of[step] = lists[which, :groups, :]
-        places = lists[which, 16 : 16 + groups, :].astype(jnp.int32)
-        row_of[step] = (places // SPAN).astype(F32)
-        lane_of[step] = lane_target(places).astype(F32)
+    shape = (groups, 128)
+    lane = lax.broadcasted_iota(jnp.int32, shape, 1)
+    lower = lane < SPAN
+    for step in range(0, lists.shape[0], 2):
+        parts = []
+        for which in (step ^ order, (step + 1) ^ order):
+            places = lists[which, 16 : 16 + groups, :].astype(jnp.int32)
+            target = (lane // (128 // QUAD)) % 2 * SPAN + places % SPAN
+            parts.append((lists[which, :groups, :], (places // SPAN).astype(F32), target.astype(F32)))
+        for out, first, second in zip((value_of, row_of, lane_of), *parts):
+            out[step] = jnp.where(lower, first, pltpu.roll(second, SPAN, 1))
+            out[step + 1] = jnp.where(lower, pltpu.roll(first, SPAN, 1), second)
 
 
 def decode_group(index, narrow, wide, value_of, row_of, lane_of):
-    left, right = [], []
-    for step in range(value_of.shape[0]):
-        value = value_of[step, index : index + 1, :]
-        wanted = row_of[step, index : index + 1, :]
-        high = value.astype(BF16).astype(F32)
-        left.append(
-            jnp.concatenate([value_at(narrow, wanted, high), value_at(narrow, wanted, value - high)], axis=0)
-        )
-        right.append(ones_at(wide, lane_of[step, index : index + 1, :]))
-    total = dot_t(jnp.concatenate(left, axis=1), jnp.concatenate(right, axis=1))
-    return total[:SPAN] + total[SPAN:]
+    pairs = []
+    for pair in range(2):
+        left, right = [], []
+        for step in range(pair, value_of.shape[0], 2):
+            value = value_of[step, index : index + 1, :]
+            wanted = row_of[step, index : index + 1, :]
+            high = value.astype(BF16).astype(F32)
+            left.append(
+                jnp.concatenate([value_at(narrow, wanted, high), value_at(narrow, wanted, value - high)], axis=0)
+            )
+            right.append(ones_at(wide, lane_of[step, index : index + 1, :]))
+        total = dot_t(jnp.concatenate(left, axis=1), jnp.concatenate(right, axis=1))
+        pairs.append(total[:SPAN] + total[SPAN:])
+    return jnp.concatenate(pairs, axis=1)
 
 
 def decode_kernel(groups, order, lists, out, value_of, row_of, lane_of):
     prepare(order[0], lists, groups, value_of, row_of, lane_of)
-    narrow, wide = counter(SPAN), counter(WIDE)
+    narrow, wide = counter(SPAN), counter(2 * SPAN)
     for index in range(groups):
         out[index * SPAN : (index + 1) * SPAN, :] = decode_group(index, narrow, wide, value_of, row_of, lane_of)
 
 
 def decode_last_kernel(groups, order, lists, held, out, squares, value_of, row_of, lane_of):
     prepare(order[0], lists, groups, value_of, row_of, lane_of)
-    narrow, wide = counter(SPAN), counter(WIDE)
+    narrow, wide = counter(SPAN), counter(2 * SPAN)
     squared = jnp.zeros((8, WIDE), F32)
     for index in range(groups):
         rows = slice(index * SPAN, (index + 1) * SPAN)
@@ -210,15 +223,24 @@
     out[...] = inverse(high, low, tables, stack, groups)
 
 
-def apply_kernel(entries, weights, update, squares, out):
-    scale = lax.rsqrt(jnp.sum(squares[...]) / entries + 1.0)
-    out[...] = weights[...] - update[...] * scale
-
-
-def call(kernel, shapes, flops, *args, spaces=None, scratch=()):
+def apply_kernel(entries, chunks, weights, update, squares, out, buf, sems):
+    total = jnp.sum(jnp.sum(squares[...], axis=0, keepdims=True), axis=1, keepdims=True)
+    scale = lax.rsqrt(total / entries + 1.0)
+    step = update.shape[0] // chunks
+    copies = []
+    for at in range(chunks):
+        rows = pl.ds(at * step, step)
+        buf[rows, :] = weights[rows, :] - update[rows, :] * scale
+        copies.append(pltpu.make_async_copy(buf.at[rows, :], out.at[rows, :], sems.at[at]))
+        copies[-1].start()
+    for copy in copies:
+        copy.wait()
+
+
+def call(kernel, shapes, flops, *args, spaces=None, scratch=(), space=pltpu.VMEM):
     spaces = spaces or {}
     specs = [pl.BlockSpec(memory_space=spaces.get(at, pltpu.VMEM)) for at in range(len(args))]
-    out_specs = jax.tree.map(lambda _: pl.BlockSpec(memory_space=pltpu.VMEM), shapes)
+    out_specs = jax.tree.map(lambda _: pl.BlockSpec(memory_space=space), shapes)
     return pl.pallas_call(
         kernel,
         out_shape=shapes,
@@ -232,35 +254,37 @@
 
 def local(replicas, parts, gradient, momentum, weights, positions):
     table = dct_table()
-    forward = jnp.asarray(operands(table))
+    columns = jnp.asarray(np.concatenate(halves(table.T), axis=0))
     backward = jnp.asarray(operands(table.T))
     height, width = weights.shape
     groups = width // WIDE
     spans, kept = positions.shape[2:]
-    chunks = 7
+    chunks = 1
     field = jax.ShapeDtypeStruct((height, width), F32)
     tall = jax.ShapeDtypeStruct((groups * SPAN, WIDE), F32)
     half = pltpu.VMEM((groups * SPAN, WIDE), BF16)
     stack = pltpu.VMEM((3 * SPAN, width), BF16)
-    message, coefs, summed = call(
+    message, summed, sides, column = call(
         functools.partial(pick_kernel, chunks),
-        (jax.ShapeDtypeStruct((1, 32, 128), F32), tall, field),
+        (
+            jax.ShapeDtypeStruct((1, 32, 128), F32),
+            field,
+            jax.ShapeDtypeStruct((groups, 2, WIDE, 128), BF16),
+            jax.ShapeDtypeStruct((groups, SPAN, 128), F32),
+        ),
         1 << 30,
         pltpu.with_memory_space_constraint(gradient, pltpu.HBM),
         pltpu.with_memory_space_constraint(momentum, pltpu.HBM),
         pltpu.with_memory_space_constraint(jnp.swapaxes(positions[0, 0], 0, 1), pltpu.HBM),
-        pltpu.with_memory_space_constraint(forward, pltpu.HBM),
+        pltpu.with_memory_space_constraint(columns, pltpu.HBM),
         spaces={0: pltpu.HBM, 1: pltpu.HBM, 2: pltpu.HBM, 3: pltpu.HBM},
         scratch=(
             pltpu.VMEM((height, width), BF16),
             pltpu.VMEM((height, width), F32),
             pltpu.VMEM((kept, spans), jnp.int32),
-            pltpu.VMEM(forward.shape, BF16),
+            pltpu.VMEM(columns.shape, BF16),
             pltpu.VMEM((spans, kept), jnp.int32),
-            stack,
-            half,
-            half,
-            pltpu.VMEM((groups, WIDE, 128), BF16),
+            pltpu.VMEM((SPAN, width), BF16),
             pltpu.SemaphoreType.DMA((2 * chunks + 2,)),
         ),
     )
@@ -268,17 +292,21 @@
         momentum_kernel,
         jax.ShapeDtypeStruct(momentum.shape, F32),
         1 << 31,
+        message,
         summed,
-        message,
-        coefs,
-        backward,
-        scratch=(half, half, stack),
+        sides,
+        column,
+        space=pltpu.HBM,
+        scratch=(pltpu.VMEM((height, width), F32), pltpu.SemaphoreType.DMA((groups,))),
     )
     held = message
     bit = 1
+    fillers = [new_momentum]
     while 2 * bit < replicas:
         other = lax.ppermute(held, "dp", [(at, at ^ bit) for at in range(replicas)])
         held = jnp.concatenate([held, other], axis=0)
+        if fillers:
+            held, _ = lax.optimization_barrier((held, fillers.pop(0)))
         bit *= 2
     order = (lax.axis_index("dp") % bit).reshape(1)
     other = lax.ppermute(held, "dp", [(at, at ^ bit) for at in range(replicas)])
@@ -308,12 +336,14 @@
         squares = squares + lax.ppermute(squares, "mp", [(at, at ^ step) for at in range(parts)])
         step *= 2
     new_weights = call(
-        functools.partial(apply_kernel, float(height * width * parts)),
+        functools.partial(apply_kernel, float(height * width * parts), 4),
         field,
         1 << 20,
         weights,
         update,
         squares,
+        space=pltpu.HBM,
+        scratch=(pltpu.VMEM((height, width), F32), pltpu.SemaphoreType.DMA((4,))),
     )
     return new_momentum, new_weights
 

time: 26.4 us -> 23.5 us (0.89)
  Pallas kernels: 10.1 us -> 6.94 us
    pallas_call x6, Pallas kernels: 10.1 us -> 6.94 us  [call(): pl.pallas_call(kernel, out_shape=shapes, in_specs=specs, out_specs=out_sp...]
    ppermute x2, waiting for transfers between devices: 0.84 us -> 1.98 us  [local(): lax.ppermute(squares, 'mp', [(at, at ^ step) for at in range(parts)])]
    ppermute x3, waiting for transfers between devices: 4.49 us -> 3.56 us  [local(): other = lax.ppermute(held, 'dp', [(at, at ^ bit) for at in range(replicas)])]
  transfers between devices with their start and end apart: 5 -> 5, of which waited for: 4 -> 5; matrix products, arithmetic and copies ran while one was open for 0% -> 0% of each run, Pallas kernels for 17% -> 14%
where the time goes in v3:
time: 23.5 us; the launch traced here: 23.3 us
  starting transfers between devices  10.1 us (43%)
  Pallas kernels  6.94 us (30%)
  waiting for transfers between devices  5.54 us (24%)
  between operations  0.7 us (3%)
    ppermute x3, starting transfers between devices, local(): other = lax.ppermute(held, 'dp', [(at, at ^ bit) for at in range(replicas)])  8.17 us
    pallas_call x6, Pallas kernels, call(): pl.pallas_call(kernel, out_shape=shapes, in_specs=specs, out_specs=out_sp...  6.94 us
    ppermute x3, waiting for transfers between devices, local(): other = lax.ppermute(held, 'dp', [(at, at ^ bit) for at in range(replicas)])  3.56 us
    ppermute x2, waiting for transfers between devices, local(): lax.ppermute(squares, 'mp', [(at, at ^ step) for at in range(parts)])  1.98 us
    ppermute x2, starting transfers between devices, local(): lax.ppermute(squares, 'mp', [(at, at ^ step) for at in range(parts)])  1.9 us
  transfers between devices with their start and end apart: 5, of which 5 were waited for; matrix products, arithmetic and copies ran while one was open for 0% of the time, Pallas kernels for 14%

profile of v3, /device:TPU:0, one launch (start us, length us, event | category | flops | bytes accessed | tf_op | source)
XLA Modules:
  0.0 23.3 jit_solution(16623482731625263328)
XLA Ops:
  0.6 1.9 %shard_map.77 = (f32[1,32,128]{2,1,0:T(8,128)S(1)}, f32[64,3584]{1,0:T(8,128)S(1)}, bf16[14,2,256,128]{3,2,1,0:T(8,128)(2,1)S(1)}, f32[14,64,128]{2,1,0:T(8,128)S(1)}) custom-call(bf16[1,64,3584]{2,1,0:T(8,128)(2,1)} %grad.1, f32[1,64,3584]{2,1,0:T(8,128)} %mom.1, s32[32,56]{1,0:T(8,128)} %bitcast.4, bf16[128,64]{1,0:T(8,128)(2,1)} %constant.23.clone.table), custom_call_target="tpu_custom_call" | custom-call | flops 1073741824 | bytes 1048576 | tf_op jit(solution)/shard_map/pallas_call | solution.py:244
  2.6 3.1 %collective-permute-start = (f32[1,32,128]{2,1,0:T(8,128)S(1)}, f32[1,32,128]{2,1,0:T(8,128)S(1)}, u32[]{:S(2)}, u32[]{:S(2)}) collective-permute-start(f32[1,32,128]{2,1,0:T(8,128)S(1)} %get-tuple-element.9.message), channel_id=1, source_target_pairs={{0,4},{4,0},{8,12},{12,8},{16,20},{20,16},{24,28},{28,24},{1,5},{5... | collective-permute-start | bytes 49160 | tf_op jit(solution)/shard_map/ppermute | solution.py:306
  5.6 1.5 %shard_map.78 = f32[1,64,3584]{2,1,0:T(8,128)} custom-call(f32[1,32,128]{2,1,0:T(8,128)S(1)} %get-tuple-element.9.message, f32[64,3584]{1,0:T(8,128)S(1)} %get-tuple-element.10.summed, bf16[14,2,256,128]{3,2,1,0:T(8,128)(2,1)S(1)} %get-tuple-element.11.sides, f32[14,64,128]{2,1,0:T(8,128)S(1)} %get-tuple-element.12.column), custom_call_target="tpu_custom_call" | custom-call | flops 2147483648 | bytes 1048576 | tf_op jit(solution)/shard_map/pallas_call | solution.py:244
  7.2 0.2 collective-permute-done
  7.4 2.1 %collective-permute-start.1 = (f32[2,32,128]{2,1,0:T(8,128)S(1)}, f32[2,32,128]{2,1,0:T(8,128)S(1)}, u32[]{:S(2)}, u32[]{:S(2)}) collective-permute-start(f32[2,32,128]{2,1,0:T(8,128)S(1)} %pad_maximum_fusion), channel_id=1, source_target_pairs={{0,8},{4,12},{8,0},{12,4},{16,24},{20,28},{24,16},{28,20},{1,9},{5... | collective-permute-start | bytes 98312 | tf_op jit(solution)/shard_map/ppermute | solution.py:306
  9.4 1.9 %collective-permute-done.1 = f32[2,32,128]{2,1,0:T(8,128)S(1)} collective-permute-done((f32[2,32,128]{2,1,0:T(8,128)S(1)}, f32[2,32,128]{2,1,0:T(8,128)S(1)}, u32[]{:S(2)}, u32[]{:S(2)}) %collective-permute-start.1) | collective-permute-done | bytes 32800 | tf_op jit(solution)/shard_map/ppermute | solution.py:306
  11.3 3.0 %collective-permute-start.2 = (f32[4,32,128]{2,1,0:T(8,128)S(1)}, f32[4,32,128]{2,1,0:T(8,128)S(1)}, u32[]{:S(2)}, u32[]{:S(2)}) collective-permute-start(f32[4,32,128]{2,1,0:T(8,128)S(1)} %constant_dynamic-update-slice_fusion.lists), channel_id=1, source_target_pairs={{0,16},{4,20},{8,24},{12,28},{16,0},{20,4},{24,8},{28,12},{1,17},{... | collective-permute-start | bytes 196616 | tf_op jit(solution)/shard_map/ppermute | solution.py:312
  14.4 0.7 %shard_map.79.held = f32[896,256]{1,0:T(8,128)S(1)} custom-call(s32[1]{0:T(128)} %bitcast.2.order, f32[4,32,128]{2,1,0:T(8,128)S(1)} %constant_dynamic-update-slice_fusion.lists), custom_call_target="tpu_custom_call" | custom-call | flops 1073741824 | bytes 1048576 | tf_op jit(solution)/shard_map/pallas_call | solution.py:244
  15.1 0.0 copy-start.1
  15.1 1.5 %collective-permute-done.2.lists = f32[4,32,128]{2,1,0:T(8,128)S(1)} collective-permute-done((f32[4,32,128]{2,1,0:T(8,128)S(1)}, f32[4,32,128]{2,1,0:T(8,128)S(1)}, u32[]{:S(2)}, u32[]{:S(2)}) %collective-permute-start.2) | collective-permute-done | bytes 65568 | tf_op jit(solution)/shard_map/ppermute | solution.py:312
  16.6 0.7 %shard_map.80 = (f32[896,256]{1,0:T(8,128)S(1)}, f32[8,128]{1,0:T(8,128)S(1)}) custom-call(s32[1]{0:T(128)} %bitcast.2.order, f32[4,32,128]{2,1,0:T(8,128)S(1)} %collective-permute-done.2.lists, f32[896,256]{1,0:T(8,128)S(1)} %shard_map.79.held), custom_call_target="tpu_custom_call" | custom-call | flops 1073741824 | bytes 1048576 | tf_op jit(solution)/shard_map/pallas_call | solution.py:244
  17.4 0.1 collective-permute-start.3
  17.4 1.2 %collective-permute-done.3 = f32[8,128]{1,0:T(8,128)S(1)} collective-permute-done((f32[8,128]{1,0:T(8,128)S(1)}, f32[8,128]{1,0:T(8,128)S(1)}, u32[]{:S(2)}, u32[]{:S(2)}) %collective-permute-start.3) | collective-permute-done | bytes 4128 | tf_op jit(solution)/shard_map/ppermute | solution.py:336
  18.6 1.8 %collective-permute-start.4 = (f32[8,128]{1,0:T(8,128)S(1)}, f32[8,128]{1,0:T(8,128)S(1)}, u32[]{:S(2)}, u32[]{:S(2)}) collective-permute-start(f32[8,128]{1,0:T(8,128)S(1)} %add.11), channel_id=1, source_target_pairs={{0,2},{1,3},{2,0},{3,1},{4,6},{5,7},{6,4},{7,5},{8,10},{9,11},{10,... | collective-permute-start | bytes 12296 | tf_op jit(solution)/shard_map/ppermute | solution.py:336
  20.4 0.0 copy-done.1
  20.4 0.0 copy-start
  20.4 0.9 %shard_map.81.update = f32[64,3584]{1,0:T(8,128)S(1)} custom-call(f32[896,256]{1,0:T(8,128)S(1)} %get-tuple-element.14.total, bf16[576,256]{1,0:T(8,128)(2,1)S(1)} %copy-done.1), custom_call_target="tpu_custom_call" | custom-call | flops 2147483648 | bytes 1048576 | tf_op jit(solution)/shard_map/pallas_call | solution.py:244
  21.4 0.8 %collective-permute-done.4 = f32[8,128]{1,0:T(8,128)S(1)} collective-permute-done((f32[8,128]{1,0:T(8,128)S(1)}, f32[8,128]{1,0:T(8,128)S(1)}, u32[]{:S(2)}, u32[]{:S(2)}) %collective-permute-start.4) | collective-permute-done | bytes 4128 | tf_op jit(solution)/shard_map/ppermute | solution.py:336
  22.2 0.0 copy-done
  22.2 1.1 %shard_map.82 = f32[64,3584]{1,0:T(8,128)} custom-call(f32[64,3584]{1,0:T(8,128)S(1)} %copy-done, f32[64,3584]{1,0:T(8,128)S(1)} %shard_map.81.update, f32[8,128]{1,0:T(8,128)S(1)} %add.12.squares), custom_call_target="tpu_custom_call" | custom-call | flops 1048576 | bytes 1048576 | tf_op jit(solution)/shard_map/pallas_call | solution.py:244
  (5 shorter events, 0.0 us)
Async XLA Ops:
  2.6 4.8 %collective-permute-start = (f32[1,32,128]{2,1,0:T(8,128)S(1)}, f32[1,32,128]{2,1,0:T(8,128)S(1)}, u32[]{:S(2)}, u32[]{:S(2)}) collective-permute-start(f32[1,32,128]{2,1,0:T(8,128)S(1)} %get-tuple-element.9.message), channel_id=1, source_target_pairs={{0,4},{4,0},{8,12},{12,8},{16,20},{20,16},{24,28},{28,24},{1,5},{5... | collective-permute-start | bytes 49160 | tf_op jit(solution)/shard_map/ppermute | solution.py:306
  7.4 4.0 %collective-permute-start.1 = (f32[2,32,128]{2,1,0:T(8,128)S(1)}, f32[2,32,128]{2,1,0:T(8,128)S(1)}, u32[]{:S(2)}, u32[]{:S(2)}) collective-permute-start(f32[2,32,128]{2,1,0:T(8,128)S(1)} %pad_maximum_fusion), channel_id=1, source_target_pairs={{0,8},{4,12},{8,0},{12,4},{16,24},{20,28},{24,16},{28,20},{1,9},{5... | collective-permute-start | bytes 98312 | tf_op jit(solution)/shard_map/ppermute | solution.py:306
  11.3 5.3 %collective-permute-start.2 = (f32[4,32,128]{2,1,0:T(8,128)S(1)}, f32[4,32,128]{2,1,0:T(8,128)S(1)}, u32[]{:S(2)}, u32[]{:S(2)}) collective-permute-start(f32[4,32,128]{2,1,0:T(8,128)S(1)} %constant_dynamic-update-slice_fusion.lists), channel_id=1, source_target_pairs={{0,16},{4,20},{8,24},{12,28},{16,0},{20,4},{24,8},{28,12},{1,17},{... | collective-permute-start | bytes 196616 | tf_op jit(solution)/shard_map/ppermute | solution.py:312
  15.1 5.3 %copy-start.1 = (bf16[576,256]{1,0:T(8,128)(2,1)S(1)}, bf16[576,256]{1,0:T(8,128)(2,1)}, u32[]{:S(2)}) copy-start(bf16[576,256]{1,0:T(8,128)(2,1)} %constant.24.clone.tables) | copy-start | bytes 884740
  17.4 1.2 %collective-permute-start.3 = (f32[8,128]{1,0:T(8,128)S(1)}, f32[8,128]{1,0:T(8,128)S(1)}, u32[]{:S(2)}, u32[]{:S(2)}) collective-permute-start(f32[8,128]{1,0:T(8,128)S(1)} %get-tuple-element.15), channel_id=1, source_target_pairs={{0,1},{1,0},{2,3},{3,2},{4,5},{5,4},{6,7},{7,6},{8,9},{9,8},{10,11... | collective-permute-start | bytes 12296 | tf_op jit(solution)/shard_map/ppermute | solution.py:336
  18.6 3.6 %collective-permute-start.4 = (f32[8,128]{1,0:T(8,128)S(1)}, f32[8,128]{1,0:T(8,128)S(1)}, u32[]{:S(2)}, u32[]{:S(2)}) collective-permute-start(f32[8,128]{1,0:T(8,128)S(1)} %add.11), channel_id=1, source_target_pairs={{0,2},{1,3},{2,0},{3,1},{4,6},{5,7},{6,4},{7,5},{8,10},{9,11},{10,... | collective-permute-start | bytes 12296 | tf_op jit(solution)/shard_map/ppermute | solution.py:336
  20.4 1.8 %copy-start = (f32[64,3584]{1,0:T(8,128)S(1)}, f32[64,3584]{1,0:T(8,128)}, u32[]{:S(2)}) copy-start(f32[64,3584]{1,0:T(8,128)} %weights.1) | copy-start | bytes 2752516

commit v4 on v3

--- a/solution.py
+++ b/solution.py
@@ -126,7 +126,7 @@
             piece = chosen[tall, at : at + 128].astype(BF16).reshape(SPAN // 16, 16, 128)
             for quarter in range(QUAD):
                 kept = jnp.where(masks[quarter][None], piece, jnp.zeros((), BF16)).reshape(SPAN, 128)
-                sides[index, half, quarter * SPAN : (quarter + 1) * SPAN, :] = kept
+                sides[index, quarter * SPAN : (quarter + 1) * SPAN, half * 128 : (half + 1) * 128] = kept
         column[index] = chosen[:SPAN, at + 128 : at + WIDE] + chosen[SPAN:, at + 128 : at + WIDE]
     for at in range(chunks):
         lanes = slice(at * step, (at + 1) * step)
@@ -137,8 +137,8 @@
         for index in range(at * step // WIDE, (at + 1) * step // WIDE):
             inner = index * WIDE - at * step
             high, low = split(total[:, inner : inner + WIDE])
-            both = dot(jnp.concatenate([high, low], axis=0), sides[index, 0])
-            values = both[:SPAN] + both[SPAN:] + dot(high, sides[index, 1])
+            both = dot(jnp.concatenate([high, low], axis=0), sides[index])
+            values = both[:SPAN, :128] + both[SPAN:, :128] + both[:SPAN, 128:]
             message[0, index : index + 1, :] = jnp.sum(values * column[index], axis=0, keepdims=True)
 
 
@@ -156,60 +156,61 @@
     for index in range(groups):
         lanes = pl.ds(index * WIDE, WIDE)
         high, low = split(column[index] * message[0, index : index + 1, :])
-        both = dot_t(jnp.concatenate([high, low], axis=0), sides[index, 0])
-        buf[:, lanes] = summed[:, lanes] - (both[:SPAN] + both[SPAN:] + dot_t(high, sides[index, 1]))
+        left = jnp.concatenate(
+            [jnp.concatenate([high, high], axis=1), jnp.concatenate([low, jnp.zeros_like(low)], axis=1)], axis=0
+        )
+        both = dot_t(left, sides[index])
+        buf[:, lanes] = summed[:, lanes] - (both[:SPAN] + both[SPAN:])
         copies.append(pltpu.make_async_copy(buf.at[:, lanes], out.at[0, :, lanes], sems.at[index]))
         copies[-1].start()
     for copy in copies:
         copy.wait()
 
 
-def prepare(order, lists, groups, value_of, row_of, lane_of):
+def prepare(order, lists, groups, tables):
     shape = (groups, 128)
     lane = lax.broadcasted_iota(jnp.int32, shape, 1)
     lower = lane < SPAN
     for step in range(0, lists.shape[0], 2):
         parts = []
         for which in (step ^ order, (step + 1) ^ order):
+            value = lists[which, :groups, :]
+            high = value.astype(BF16).astype(F32)
             places = lists[which, 16 : 16 + groups, :].astype(jnp.int32)
             target = (lane // (128 // QUAD)) % 2 * SPAN + places % SPAN
-            parts.append((lists[which, :groups, :], (places // SPAN).astype(F32), target.astype(F32)))
-        for out, first, second in zip((value_of, row_of, lane_of), *parts):
+            parts.append((high, value - high, (places // SPAN).astype(F32), target.astype(F32)))
+        for out, first, second in zip(tables, *parts):
             out[step] = jnp.where(lower, first, pltpu.roll(second, SPAN, 1))
             out[step + 1] = jnp.where(lower, pltpu.roll(first, SPAN, 1), second)
 
 
-def decode_group(index, narrow, wide, value_of, row_of, lane_of):
+def decode_group(index, narrow, wide, tables):
     pairs = []
     for pair in range(2):
         left, right = [], []
-        for step in range(pair, value_of.shape[0], 2):
-            value = value_of[step, index : index + 1, :]
-            wanted = row_of[step, index : index + 1, :]
-            high = value.astype(BF16).astype(F32)
-            left.append(
-                jnp.concatenate([value_at(narrow, wanted, high), value_at(narrow, wanted, value - high)], axis=0)
-            )
-            right.append(ones_at(wide, lane_of[step, index : index + 1, :]))
+        for step in range(pair, tables[0].shape[0], 2):
+            high, low, row, target = (table[step, index : index + 1, :] for table in tables)
+            left.append(jnp.concatenate([value_at(narrow, row, high), value_at(narrow, row, low)], axis=0))
+            right.append(ones_at(wide, target))
         total = dot_t(jnp.concatenate(left, axis=1), jnp.concatenate(right, axis=1))
         pairs.append(total[:SPAN] + total[SPAN:])
     return jnp.concatenate(pairs, axis=1)
 
 
-def decode_kernel(groups, order, lists, out, value_of, row_of, lane_of):
-    prepare(order[0], lists, groups, value_of, row_of, lane_of)
+def decode_kernel(groups, order, lists, out, *tables):
+    prepare(order[0], lists, groups, tables)
     narrow, wide = counter(SPAN), counter(2 * SPAN)
     for index in range(groups):
-        out[index * SPAN : (index + 1) * SPAN, :] = decode_group(index, narrow, wide, value_of, row_of, lane_of)
-
-
-def decode_last_kernel(groups, order, lists, held, out, squares, value_of, row_of, lane_of):
-    prepare(order[0], lists, groups, value_of, row_of, lane_of)
+        out[index * SPAN : (index + 1) * SPAN, :] = decode_group(index, narrow, wide, tables)
+
+
+def decode_last_kernel(groups, order, lists, held, out, squares, *tables):
+    prepare(order[0], lists, groups, tables)
     narrow, wide = counter(SPAN), counter(2 * SPAN)
     squared = jnp.zeros((8, WIDE), F32)
     for index in range(groups):
         rows = slice(index * SPAN, (index + 1) * SPAN)
-        total = held[rows, :] + decode_group(index, narrow, wide, value_of, row_of, lane_of)
+        total = held[rows, :] + decode_group(index, narrow, wide, tables)
         out[rows, :] = total
         squared = squared + jnp.sum((total * total).reshape(8, 8, WIDE), axis=0)
     squares[...] = squared[:, :128] + squared[:, 128:]
@@ -269,7 +270,7 @@
         (
             jax.ShapeDtypeStruct((1, 32, 128), F32),
             field,
-            jax.ShapeDtypeStruct((groups, 2, WIDE, 128), BF16),
+            jax.ShapeDtypeStruct((groups, WIDE, 2 * 128), BF16),
             jax.ShapeDtypeStruct((groups, SPAN, 128), F32),
         ),
         1 << 30,
@@ -310,7 +311,7 @@
         bit *= 2
     order = (lax.axis_index("dp") % bit).reshape(1)
     other = lax.ppermute(held, "dp", [(at, at ^ bit) for at in range(replicas)])
-    tables = tuple(pltpu.VMEM((bit, groups, 128), F32) for _ in range(3))
+    tables = tuple(pltpu.VMEM((bit, groups, 128), F32) for _ in range(4))
     own_total = call(
         functools.partial(decode_kernel, groups),
         tall,
@@ -333,7 +334,8 @@
     update = call(update_kernel, field, 1 << 31, total, backward, scratch=(half, half, stack))
     step = 1
     while step < parts:
-        squares = squares + lax.ppermute(squares, "mp", [(at, at ^ step) for at in range(parts)])
+        flip = 2 * step - 1
+        squares = squares + lax.ppermute(squares, "mp", [(at, at ^ flip) for at in range(parts)])
         step *= 2
     new_weights = call(
         functools.partial(apply_kernel, float(height * width * parts), 4),

time: 23.5 us -> 22.9 us (0.974)
  waiting for transfers between devices: 5.54 us -> 5.2 us
  starting transfers between devices: 10.1 us -> 9.84 us
    ppermute x2, waiting for transfers between devices: 1.98 us -> 1.63 us  [local(): lax.ppermute(squares, 'mp', [(at, at ^ flip) for at in range(parts)])]
where the time goes in v4:
time: 22.9 us; the launch traced here: 22.6 us
  starting transfers between devices  9.84 us (43%)
  Pallas kernels  6.85 us (30%)
  waiting for transfers between devices  5.2 us (23%)
  between operations  0.7 us (3%)
    ppermute x3, starting transfers between devices, local(): other = lax.ppermute(held, 'dp', [(at, at ^ bit) for at in range(replicas)])  8.17 us
    pallas_call x6, Pallas kernels, call(): pl.pallas_call(kernel, out_shape=shapes, in_specs=specs, out_specs=out_sp...  6.85 us
    ppermute x3, waiting for transfers between devices, local(): other = lax.ppermute(held, 'dp', [(at, at ^ bit) for at in range(replicas)])  3.56 us
    ppermute x2, starting transfers between devices, local(): lax.ppermute(squares, 'mp', [(at, at ^ flip) for at in range(parts)])  1.67 us
    ppermute x2, waiting for transfers between devices, local(): lax.ppermute(squares, 'mp', [(at, at ^ flip) for at in range(parts)])  1.63 us
  transfers between devices with their start and end apart: 5, of which 5 were waited for; matrix products, arithmetic and copies ran while one was open for 0% of the time, Pallas kernels for 14%

profile of v4, /device:TPU:0, one launch (start us, length us, event | category | flops | bytes accessed | tf_op | source)
XLA Modules:
  0.0 22.6 jit_solution(15645387616169254163)
XLA Ops:
  0.6 1.8 %shard_map.77 = (f32[1,32,128]{2,1,0:T(8,128)S(1)}, f32[64,3584]{1,0:T(8,128)S(1)}, bf16[14,256,256]{2,1,0:T(8,128)(2,1)S(1)}, f32[14,64,128]{2,1,0:T(8,128)S(1)}) custom-call(bf16[1,64,3584]{2,1,0:T(8,128)(2,1)} %grad.1, f32[1,64,3584]{2,1,0:T(8,128)} %mom.1, s32[32,56]{1,0:T(8,128)} %bitcast.4, bf16[128,64]{1,0:T(8,128)(2,1)} %constant.23.clone.table), custom_call_target="tpu_custom_call" | custom-call | flops 1073741824 | bytes 1048576 | tf_op jit(solution)/shard_map/pallas_call | solution.py:245
  2.5 3.1 %collective-permute-start = (f32[1,32,128]{2,1,0:T(8,128)S(1)}, f32[1,32,128]{2,1,0:T(8,128)S(1)}, u32[]{:S(2)}, u32[]{:S(2)}) collective-permute-start(f32[1,32,128]{2,1,0:T(8,128)S(1)} %get-tuple-element.9.message), channel_id=1, source_target_pairs={{0,4},{4,0},{8,12},{12,8},{16,20},{20,16},{24,28},{28,24},{1,5},{5... | collective-permute-start | bytes 49160 | tf_op jit(solution)/shard_map/ppermute | solution.py:307
  5.5 1.5 %shard_map.78 = f32[1,64,3584]{2,1,0:T(8,128)} custom-call(f32[1,32,128]{2,1,0:T(8,128)S(1)} %get-tuple-element.9.message, f32[64,3584]{1,0:T(8,128)S(1)} %get-tuple-element.10.summed, bf16[14,256,256]{2,1,0:T(8,128)(2,1)S(1)} %get-tuple-element.11.sides, f32[14,64,128]{2,1,0:T(8,128)S(1)} %get-tuple-element.12.column), custom_call_target="tpu_custom_call" | custom-call | flops 2147483648 | bytes 1048576 | tf_op jit(solution)/shard_map/pallas_call | solution.py:245
  7.1 0.2 collective-permute-done
  7.3 2.1 %collective-permute-start.1 = (f32[2,32,128]{2,1,0:T(8,128)S(1)}, f32[2,32,128]{2,1,0:T(8,128)S(1)}, u32[]{:S(2)}, u32[]{:S(2)}) collective-permute-start(f32[2,32,128]{2,1,0:T(8,128)S(1)} %pad_maximum_fusion), channel_id=1, source_target_pairs={{0,8},{4,12},{8,0},{12,4},{16,24},{20,28},{24,16},{28,20},{1,9},{5... | collective-permute-start | bytes 98312 | tf_op jit(solution)/shard_map/ppermute | solution.py:307
  9.3 1.9 %collective-permute-done.1 = f32[2,32,128]{2,1,0:T(8,128)S(1)} collective-permute-done((f32[2,32,128]{2,1,0:T(8,128)S(1)}, f32[2,32,128]{2,1,0:T(8,128)S(1)}, u32[]{:S(2)}, u32[]{:S(2)}) %collective-permute-start.1) | collective-permute-done | bytes 32800 | tf_op jit(solution)/shard_map/ppermute | solution.py:307
  11.2 3.0 %collective-permute-start.2 = (f32[4,32,128]{2,1,0:T(8,128)S(1)}, f32[4,32,128]{2,1,0:T(8,128)S(1)}, u32[]{:S(2)}, u32[]{:S(2)}) collective-permute-start(f32[4,32,128]{2,1,0:T(8,128)S(1)} %constant_dynamic-update-slice_fusion.lists), channel_id=1, source_target_pairs={{0,16},{4,20},{8,24},{12,28},{16,0},{20,4},{24,8},{28,12},{1,17},{... | collective-permute-start | bytes 196616 | tf_op jit(solution)/shard_map/ppermute | solution.py:313
  14.3 0.7 %shard_map.79.held = f32[896,256]{1,0:T(8,128)S(1)} custom-call(s32[1]{0:T(128)} %bitcast.2.order, f32[4,32,128]{2,1,0:T(8,128)S(1)} %constant_dynamic-update-slice_fusion.lists), custom_call_target="tpu_custom_call" | custom-call | flops 1073741824 | bytes 1048576 | tf_op jit(solution)/shard_map/pallas_call | solution.py:245
  15.0 0.0 copy-start.1
  15.0 1.5 %collective-permute-done.2.lists = f32[4,32,128]{2,1,0:T(8,128)S(1)} collective-permute-done((f32[4,32,128]{2,1,0:T(8,128)S(1)}, f32[4,32,128]{2,1,0:T(8,128)S(1)}, u32[]{:S(2)}, u32[]{:S(2)}) %collective-permute-start.2) | collective-permute-done | bytes 65568 | tf_op jit(solution)/shard_map/ppermute | solution.py:313
  16.5 0.8 %shard_map.80 = (f32[896,256]{1,0:T(8,128)S(1)}, f32[8,128]{1,0:T(8,128)S(1)}) custom-call(s32[1]{0:T(128)} %bitcast.2.order, f32[4,32,128]{2,1,0:T(8,128)S(1)} %collective-permute-done.2.lists, f32[896,256]{1,0:T(8,128)S(1)} %shard_map.79.held), custom_call_target="tpu_custom_call" | custom-call | flops 1073741824 | bytes 1048576 | tf_op jit(solution)/shard_map/pallas_call | solution.py:245
  17.3 0.1 collective-permute-start.3
  17.3 1.2 %collective-permute-done.3 = f32[8,128]{1,0:T(8,128)S(1)} collective-permute-done((f32[8,128]{1,0:T(8,128)S(1)}, f32[8,128]{1,0:T(8,128)S(1)}, u32[]{:S(2)}, u32[]{:S(2)}) %collective-permute-start.3) | collective-permute-done | bytes 4128 | tf_op jit(solution)/shard_map/ppermute | solution.py:338
  18.5 1.6 %collective-permute-start.4 = (f32[8,128]{1,0:T(8,128)S(1)}, f32[8,128]{1,0:T(8,128)S(1)}, u32[]{:S(2)}, u32[]{:S(2)}) collective-permute-start(f32[8,128]{1,0:T(8,128)S(1)} %add.11), channel_id=1, source_target_pairs={{0,3},{1,2},{2,1},{3,0},{4,7},{5,6},{6,5},{7,4},{8,11},{9,10},{10,... | collective-permute-start | bytes 12296 | tf_op jit(solution)/shard_map/ppermute | solution.py:338
  20.1 0.0 copy-done.1
  20.1 0.0 copy-start
  20.1 0.9 %shard_map.81.update = f32[64,3584]{1,0:T(8,128)S(1)} custom-call(f32[896,256]{1,0:T(8,128)S(1)} %get-tuple-element.14.total, bf16[576,256]{1,0:T(8,128)(2,1)S(1)} %copy-done.1), custom_call_target="tpu_custom_call" | custom-call | flops 2147483648 | bytes 1048576 | tf_op jit(solution)/shard_map/pallas_call | solution.py:245
  21.1 0.5 %collective-permute-done.4 = f32[8,128]{1,0:T(8,128)S(1)} collective-permute-done((f32[8,128]{1,0:T(8,128)S(1)}, f32[8,128]{1,0:T(8,128)S(1)}, u32[]{:S(2)}, u32[]{:S(2)}) %collective-permute-start.4) | collective-permute-done | bytes 4128 | tf_op jit(solution)/shard_map/ppermute | solution.py:338
  21.5 0.0 copy-done
  21.5 1.1 %shard_map.82 = f32[64,3584]{1,0:T(8,128)} custom-call(f32[64,3584]{1,0:T(8,128)S(1)} %copy-done, f32[64,3584]{1,0:T(8,128)S(1)} %shard_map.81.update, f32[8,128]{1,0:T(8,128)S(1)} %add.12.squares), custom_call_target="tpu_custom_call" | custom-call | flops 1048576 | bytes 1048576 | tf_op jit(solution)/shard_map/pallas_call | solution.py:245
  (5 shorter events, 0.0 us)
Async XLA Ops:
  2.5 4.8 %collective-permute-start = (f32[1,32,128]{2,1,0:T(8,128)S(1)}, f32[1,32,128]{2,1,0:T(8,128)S(1)}, u32[]{:S(2)}, u32[]{:S(2)}) collective-permute-start(f32[1,32,128]{2,1,0:T(8,128)S(1)} %get-tuple-element.9.message), channel_id=1, source_target_pairs={{0,4},{4,0},{8,12},{12,8},{16,20},{20,16},{24,28},{28,24},{1,5},{5... | collective-permute-start | bytes 49160 | tf_op jit(solution)/shard_map/ppermute | solution.py:307
  7.3 4.0 %collective-permute-start.1 = (f32[2,32,128]{2,1,0:T(8,128)S(1)}, f32[2,32,128]{2,1,0:T(8,128)S(1)}, u32[]{:S(2)}, u32[]{:S(2)}) collective-permute-start(f32[2,32,128]{2,1,0:T(8,128)S(1)} %pad_maximum_fusion), channel_id=1, source_target_pairs={{0,8},{4,12},{8,0},{12,4},{16,24},{20,28},{24,16},{28,20},{1,9},{5... | collective-permute-start | bytes 98312 | tf_op jit(solution)/shard_map/ppermute | solution.py:307
  11.2 5.3 %collective-permute-start.2 = (f32[4,32,128]{2,1,0:T(8,128)S(1)}, f32[4,32,128]{2,1,0:T(8,128)S(1)}, u32[]{:S(2)}, u32[]{:S(2)}) collective-permute-start(f32[4,32,128]{2,1,0:T(8,128)S(1)} %constant_dynamic-update-slice_fusion.lists), channel_id=1, source_target_pairs={{0,16},{4,20},{8,24},{12,28},{16,0},{20,4},{24,8},{28,12},{1,17},{... | collective-permute-start | bytes 196616 | tf_op jit(solution)/shard_map/ppermute | solution.py:313
  15.0 5.1 %copy-start.1 = (bf16[576,256]{1,0:T(8,128)(2,1)S(1)}, bf16[576,256]{1,0:T(8,128)(2,1)}, u32[]{:S(2)}) copy-start(bf16[576,256]{1,0:T(8,128)(2,1)} %constant.24.clone.tables) | copy-start | bytes 884740
  17.3 1.2 %collective-permute-start.3 = (f32[8,128]{1,0:T(8,128)S(1)}, f32[8,128]{1,0:T(8,128)S(1)}, u32[]{:S(2)}, u32[]{:S(2)}) collective-permute-start(f32[8,128]{1,0:T(8,128)S(1)} %get-tuple-element.15), channel_id=1, source_target_pairs={{0,1},{1,0},{2,3},{3,2},{4,5},{5,4},{6,7},{7,6},{8,9},{9,8},{10,11... | collective-permute-start | bytes 12296 | tf_op jit(solution)/shard_map/ppermute | solution.py:338
  18.5 3.0 %collective-permute-start.4 = (f32[8,128]{1,0:T(8,128)S(1)}, f32[8,128]{1,0:T(8,128)S(1)}, u32[]{:S(2)}, u32[]{:S(2)}) collective-permute-start(f32[8,128]{1,0:T(8,128)S(1)} %add.11), channel_id=1, source_target_pairs={{0,3},{1,2},{2,1},{3,0},{4,7},{5,6},{6,5},{7,4},{8,11},{9,10},{10,... | collective-permute-start | bytes 12296 | tf_op jit(solution)/shard_map/ppermute | solution.py:338
  20.1 1.4 %copy-start = (f32[64,3584]{1,0:T(8,128)S(1)}, f32[64,3584]{1,0:T(8,128)}, u32[]{:S(2)}) copy-start(f32[64,3584]{1,0:T(8,128)} %weights.1) | copy-start | bytes 2752516

commit v5 on v4

--- a/solution.py
+++ b/solution.py
@@ -11,6 +11,7 @@
 SPAN = 64
 QUAD = 4
 WIDE = SPAN * QUAD
+SHIFT = 6
 F32 = jnp.float32
 BF16 = jnp.bfloat16
 VMEM_LIMIT = 24 * 1024 * 1024
@@ -67,7 +68,7 @@
 
 def lane_target(place):
     quarter = lax.broadcasted_iota(jnp.int32, place.shape, 1) // (128 // QUAD)
-    return quarter * SPAN + place % SPAN
+    return quarter * SPAN + (place & (SPAN - 1))
 
 
 def counter(size):
@@ -112,8 +113,8 @@
     turned[...] = jnp.transpose(p_buf[...])
     places = jnp.concatenate([turned[pl.ds(at, groups, stride=QUAD), :] for at in range(QUAD)], axis=1)
     message[0, 16 : 16 + groups, :] = places.astype(F32)
-    row_of = (places // SPAN).astype(F32)
-    column_of = (places % SPAN).astype(F32)
+    row_of = (places >> SHIFT).astype(F32)
+    column_of = ((places & (SPAN - 1))).astype(F32)
     for index in range(groups):
         hots[:, index * WIDE : index * WIDE + 128] = ones_at(narrow, column_of[index : index + 1])
         hots[:, index * WIDE + 128 : (index + 1) * WIDE] = ones_at(narrow, row_of[index : index + 1])
@@ -167,18 +168,20 @@
         copy.wait()
 
 
-def prepare(order, lists, groups, tables):
+def prepare(lists, groups, tables):
+    order = lax.axis_index("dp") & (lists.shape[0] - 1)
     shape = (groups, 128)
     lane = lax.broadcasted_iota(jnp.int32, shape, 1)
     lower = lane < SPAN
+    span = ((lane >> 5) & 1) * SPAN
     for step in range(0, lists.shape[0], 2):
         parts = []
         for which in (step ^ order, (step + 1) ^ order):
             value = lists[which, :groups, :]
             high = value.astype(BF16).astype(F32)
             places = lists[which, 16 : 16 + groups, :].astype(jnp.int32)
-            target = (lane // (128 // QUAD)) % 2 * SPAN + places % SPAN
-            parts.append((high, value - high, (places // SPAN).astype(F32), target.astype(F32)))
+            target = span + (places & (SPAN - 1))
+            parts.append((high, value - high, (places >> SHIFT).astype(F32), target.astype(F32)))
         for out, first, second in zip(tables, *parts):
             out[step] = jnp.where(lower, first, pltpu.roll(second, SPAN, 1))
             out[step + 1] = jnp.where(lower, pltpu.roll(first, SPAN, 1), second)
@@ -197,15 +200,15 @@
     return jnp.concatenate(pairs, axis=1)
 
 
-def decode_kernel(groups, order, lists, out, *tables):
-    prepare(order[0], lists, groups, tables)
+def decode_kernel(groups, lists, out, *tables):
+    prepare(lists, groups, tables)
     narrow, wide = counter(SPAN), counter(2 * SPAN)
     for index in range(groups):
         out[index * SPAN : (index + 1) * SPAN, :] = decode_group(index, narrow, wide, tables)
 
 
-def decode_last_kernel(groups, order, lists, held, out, squares, *tables):
-    prepare(order[0], lists, groups, tables)
+def decode_last_kernel(groups, lists, held, out, squares, *tables):
+    prepare(lists, groups, tables)
     narrow, wide = counter(SPAN), counter(2 * SPAN)
     squared = jnp.zeros((8, WIDE), F32)
     for index in range(groups):
@@ -309,26 +312,21 @@
         if fillers:
             held, _ = lax.optimization_barrier((held, fillers.pop(0)))
         bit *= 2
-    order = (lax.axis_index("dp") % bit).reshape(1)
     other = lax.ppermute(held, "dp", [(at, at ^ bit) for at in range(replicas)])
     tables = tuple(pltpu.VMEM((bit, groups, 128), F32) for _ in range(4))
     own_total = call(
         functools.partial(decode_kernel, groups),
         tall,
         1 << 30,
-        order,
         held,
-        spaces={0: pltpu.SMEM},
         scratch=tables,
     )
     total, squares = call(
         functools.partial(decode_last_kernel, groups),
         (tall, jax.ShapeDtypeStruct((8, 128), F32)),
         1 << 30,
-        order,
         other,
         own_total,
-        spaces={0: pltpu.SMEM},
         scratch=tables,
     )
     update = call(update_kernel, field, 1 << 31, total, backward, scratch=(half, half, stack))

time: 22.9 us -> 22.8 us (level)
  no operation moved by 1% of the time
where the time goes in v5:
time: 22.8 us; the launch traced here: 22.6 us
  starting transfers between devices  9.83 us (43%)
  Pallas kernels  6.82 us (30%)
  waiting for transfers between devices  5.23 us (23%)
  between operations  0.69 us (3%)
    ppermute x3, starting transfers between devices, local(): other = lax.ppermute(held, 'dp', [(at, at ^ bit) for at in range(replicas)])  8.17 us
    pallas_call x6, Pallas kernels, call(): pl.pallas_call(kernel, out_shape=shapes, in_specs=specs, out_specs=out_sp...  6.82 us
    ppermute x3, waiting for transfers between devices, local(): other = lax.ppermute(held, 'dp', [(at, at ^ bit) for at in range(replicas)])  3.59 us
    ppermute x2, starting transfers between devices, local(): lax.ppermute(squares, 'mp', [(at, at ^ flip) for at in range(parts)])  1.66 us
    ppermute x2, waiting for transfers between devices, local(): lax.ppermute(squares, 'mp', [(at, at ^ flip) for at in range(parts)])  1.64 us
  transfers between devices with their start and end apart: 5, of which 5 were waited for; matrix products, arithmetic and copies ran while one was open for 0% of the time, Pallas kernels for 14%

profile of v5, /device:TPU:0, one launch (start us, length us, event | category | flops | bytes accessed | tf_op | source)
XLA Modules:
  0.0 22.6 jit_solution(17912159932140029743)
XLA Ops:
  0.6 1.8 %shard_map.77 = (f32[1,32,128]{2,1,0:T(8,128)S(1)}, f32[64,3584]{1,0:T(8,128)S(1)}, bf16[14,256,256]{2,1,0:T(8,128)(2,1)S(1)}, f32[14,64,128]{2,1,0:T(8,128)S(1)}) custom-call(bf16[1,64,3584]{2,1,0:T(8,128)(2,1)} %grad.1, f32[1,64,3584]{2,1,0:T(8,128)} %mom.1, s32[32,56]{1,0:T(8,128)} %bitcast.3, bf16[128,64]{1,0:T(8,128)(2,1)} %constant.4.clone.table), custom_call_target="tpu_custom_call" | custom-call | flops 1073741824 | bytes 1048576 | tf_op jit(solution)/shard_map/pallas_call | solution.py:248
  2.5 3.1 %collective-permute-start = (f32[1,32,128]{2,1,0:T(8,128)S(1)}, f32[1,32,128]{2,1,0:T(8,128)S(1)}, u32[]{:S(2)}, u32[]{:S(2)}) collective-permute-start(f32[1,32,128]{2,1,0:T(8,128)S(1)} %get-tuple-element.9.message), channel_id=1, source_target_pairs={{0,4},{4,0},{8,12},{12,8},{16,20},{20,16},{24,28},{28,24},{1,5},{5... | collective-permute-start | bytes 49160 | tf_op jit(solution)/shard_map/ppermute | solution.py:310
  5.5 1.5 %shard_map.78 = f32[1,64,3584]{2,1,0:T(8,128)} custom-call(f32[1,32,128]{2,1,0:T(8,128)S(1)} %get-tuple-element.9.message, f32[64,3584]{1,0:T(8,128)S(1)} %get-tuple-element.10.summed, bf16[14,256,256]{2,1,0:T(8,128)(2,1)S(1)} %get-tuple-element.11.sides, f32[14,64,128]{2,1,0:T(8,128)S(1)} %get-tuple-element.12.column), custom_call_target="tpu_custom_call" | custom-call | flops 2147483648 | bytes 1048576 | tf_op jit(solution)/shard_map/pallas_call | solution.py:248
  7.0 0.2 collective-permute-done
  7.2 2.1 %collective-permute-start.1 = (f32[2,32,128]{2,1,0:T(8,128)S(1)}, f32[2,32,128]{2,1,0:T(8,128)S(1)}, u32[]{:S(2)}, u32[]{:S(2)}) collective-permute-start(f32[2,32,128]{2,1,0:T(8,128)S(1)} %pad_maximum_fusion), channel_id=1, source_target_pairs={{0,8},{4,12},{8,0},{12,4},{16,24},{20,28},{24,16},{28,20},{1,9},{5... | collective-permute-start | bytes 98312 | tf_op jit(solution)/shard_map/ppermute | solution.py:310
  9.3 1.9 %collective-permute-done.1 = f32[2,32,128]{2,1,0:T(8,128)S(1)} collective-permute-done((f32[2,32,128]{2,1,0:T(8,128)S(1)}, f32[2,32,128]{2,1,0:T(8,128)S(1)}, u32[]{:S(2)}, u32[]{:S(2)}) %collective-permute-start.1) | collective-permute-done | bytes 32800 | tf_op jit(solution)/shard_map/ppermute | solution.py:310
  11.2 3.0 %collective-permute-start.2 = (f32[4,32,128]{2,1,0:T(8,128)S(1)}, f32[4,32,128]{2,1,0:T(8,128)S(1)}, u32[]{:S(2)}, u32[]{:S(2)}) collective-permute-start(f32[4,32,128]{2,1,0:T(8,128)S(1)} %constant_dynamic-update-slice_fusion.lists), channel_id=1, source_target_pairs={{0,16},{4,20},{8,24},{12,28},{16,0},{20,4},{24,8},{28,12},{1,17},{... | collective-permute-start | bytes 196616 | tf_op jit(solution)/shard_map/ppermute | solution.py:315
  14.3 0.7 %shard_map.79.held = f32[896,256]{1,0:T(8,128)S(1)} custom-call(f32[4,32,128]{2,1,0:T(8,128)S(1)} %constant_dynamic-update-slice_fusion.lists), custom_call_target="tpu_custom_call" | custom-call | flops 1073741824 | bytes 1048576 | tf_op jit(solution)/shard_map/pallas_call | solution.py:248
  15.0 0.0 copy-start.1
  15.0 1.5 %collective-permute-done.2.lists = f32[4,32,128]{2,1,0:T(8,128)S(1)} collective-permute-done((f32[4,32,128]{2,1,0:T(8,128)S(1)}, f32[4,32,128]{2,1,0:T(8,128)S(1)}, u32[]{:S(2)}, u32[]{:S(2)}) %collective-permute-start.2) | collective-permute-done | bytes 65568 | tf_op jit(solution)/shard_map/ppermute | solution.py:315
  16.5 0.7 %shard_map.80 = (f32[896,256]{1,0:T(8,128)S(1)}, f32[8,128]{1,0:T(8,128)S(1)}) custom-call(f32[4,32,128]{2,1,0:T(8,128)S(1)} %collective-permute-done.2.lists, f32[896,256]{1,0:T(8,128)S(1)} %shard_map.79.held), custom_call_target="tpu_custom_call" | custom-call | flops 1073741824 | bytes 1048576 | tf_op jit(solution)/shard_map/pallas_call | solution.py:248
  17.3 0.1 collective-permute-start.3
  17.3 1.2 %collective-permute-done.3 = f32[8,128]{1,0:T(8,128)S(1)} collective-permute-done((f32[8,128]{1,0:T(8,128)S(1)}, f32[8,128]{1,0:T(8,128)S(1)}, u32[]{:S(2)}, u32[]{:S(2)}) %collective-permute-start.3) | collective-permute-done | bytes 4128 | tf_op jit(solution)/shard_map/ppermute | solution.py:336
  18.5 1.6 %collective-permute-start.4 = (f32[8,128]{1,0:T(8,128)S(1)}, f32[8,128]{1,0:T(8,128)S(1)}, u32[]{:S(2)}, u32[]{:S(2)}) collective-permute-start(f32[8,128]{1,0:T(8,128)S(1)} %add.6), channel_id=1, source_target_pairs={{0,3},{1,2},{2,1},{3,0},{4,7},{5,6},{6,5},{7,4},{8,11},{9,10},{10,... | collective-permute-start | bytes 12296 | tf_op jit(solution)/shard_map/ppermute | solution.py:336
  20.1 0.0 copy-done.1
  20.1 0.0 copy-start
  20.1 0.9 %shard_map.81.update = f32[64,3584]{1,0:T(8,128)S(1)} custom-call(f32[896,256]{1,0:T(8,128)S(1)} %get-tuple-element.14.total, bf16[576,256]{1,0:T(8,128)(2,1)S(1)} %copy-done.1), custom_call_target="tpu_custom_call" | custom-call | flops 2147483648 | bytes 1048576 | tf_op jit(solution)/shard_map/pallas_call | solution.py:248
  21.0 0.5 %collective-permute-done.4 = f32[8,128]{1,0:T(8,128)S(1)} collective-permute-done((f32[8,128]{1,0:T(8,128)S(1)}, f32[8,128]{1,0:T(8,128)S(1)}, u32[]{:S(2)}, u32[]{:S(2)}) %collective-permute-start.4) | collective-permute-done | bytes 4128 | tf_op jit(solution)/shard_map/ppermute | solution.py:336
  21.5 0.0 copy-done
  21.5 1.1 %shard_map.82 = f32[64,3584]{1,0:T(8,128)} custom-call(f32[64,3584]{1,0:T(8,128)S(1)} %copy-done, f32[64,3584]{1,0:T(8,128)S(1)} %shard_map.81.update, f32[8,128]{1,0:T(8,128)S(1)} %add.7.squares), custom_call_target="tpu_custom_call" | custom-call | flops 1048576 | bytes 1048576 | tf_op jit(solution)/shard_map/pallas_call | solution.py:248
  (5 shorter events, 0.0 us)
Async XLA Ops:
  2.5 4.8 %collective-permute-start = (f32[1,32,128]{2,1,0:T(8,128)S(1)}, f32[1,32,128]{2,1,0:T(8,128)S(1)}, u32[]{:S(2)}, u32[]{:S(2)}) collective-permute-start(f32[1,32,128]{2,1,0:T(8,128)S(1)} %get-tuple-element.9.message), channel_id=1, source_target_pairs={{0,4},{4,0},{8,12},{12,8},{16,20},{20,16},{24,28},{28,24},{1,5},{5... | collective-permute-start | bytes 49160 | tf_op jit(solution)/shard_map/ppermute | solution.py:310
  7.2 4.0 %collective-permute-start.1 = (f32[2,32,128]{2,1,0:T(8,128)S(1)}, f32[2,32,128]{2,1,0:T(8,128)S(1)}, u32[]{:S(2)}, u32[]{:S(2)}) collective-permute-start(f32[2,32,128]{2,1,0:T(8,128)S(1)} %pad_maximum_fusion), channel_id=1, source_target_pairs={{0,8},{4,12},{8,0},{12,4},{16,24},{20,28},{24,16},{28,20},{1,9},{5... | collective-permute-start | bytes 98312 | tf_op jit(solution)/shard_map/ppermute | solution.py:310
  11.2 5.3 %collective-permute-start.2 = (f32[4,32,128]{2,1,0:T(8,128)S(1)}, f32[4,32,128]{2,1,0:T(8,128)S(1)}, u32[]{:S(2)}, u32[]{:S(2)}) collective-permute-start(f32[4,32,128]{2,1,0:T(8,128)S(1)} %constant_dynamic-update-slice_fusion.lists), channel_id=1, source_target_pairs={{0,16},{4,20},{8,24},{12,28},{16,0},{20,4},{24,8},{28,12},{1,17},{... | collective-permute-start | bytes 196616 | tf_op jit(solution)/shard_map/ppermute | solution.py:315
  15.0 5.1 %copy-start.1 = (bf16[576,256]{1,0:T(8,128)(2,1)S(1)}, bf16[576,256]{1,0:T(8,128)(2,1)}, u32[]{:S(2)}) copy-start(bf16[576,256]{1,0:T(8,128)(2,1)} %constant.5.clone.tables) | copy-start | bytes 884740
  17.3 1.2 %collective-permute-start.3 = (f32[8,128]{1,0:T(8,128)S(1)}, f32[8,128]{1,0:T(8,128)S(1)}, u32[]{:S(2)}, u32[]{:S(2)}) collective-permute-start(f32[8,128]{1,0:T(8,128)S(1)} %get-tuple-element.15), channel_id=1, source_target_pairs={{0,1},{1,0},{2,3},{3,2},{4,5},{5,4},{6,7},{7,6},{8,9},{9,8},{10,11... | collective-permute-start | bytes 12296 | tf_op jit(solution)/shard_map/ppermute | solution.py:336
  18.5 3.0 %collective-permute-start.4 = (f32[8,128]{1,0:T(8,128)S(1)}, f32[8,128]{1,0:T(8,128)S(1)}, u32[]{:S(2)}, u32[]{:S(2)}) collective-permute-start(f32[8,128]{1,0:T(8,128)S(1)} %add.6), channel_id=1, source_target_pairs={{0,3},{1,2},{2,1},{3,0},{4,7},{5,6},{6,5},{7,4},{8,11},{9,10},{10,... | collective-permute-start | bytes 12296 | tf_op jit(solution)/shard_map/ppermute | solution.py:336
  20.1 1.4 %copy-start = (f32[64,3584]{1,0:T(8,128)S(1)}, f32[64,3584]{1,0:T(8,128)}, u32[]{:S(2)}) copy-start(f32[64,3584]{1,0:T(8,128)} %weights.1) | copy-start | bytes 2752516

commit v6 on v5

--- a/solution.py
+++ b/solution.py
@@ -330,11 +330,10 @@
         scratch=tables,
     )
     update = call(update_kernel, field, 1 << 31, total, backward, scratch=(half, half, stack))
-    step = 1
-    while step < parts:
-        flip = 2 * step - 1
+    for step in reversed(range(1, parts.bit_length())):
+        flip = 2**step - 1
         squares = squares + lax.ppermute(squares, "mp", [(at, at ^ flip) for at in range(parts)])
-        step *= 2
+        squares, update = lax.optimization_barrier((squares, update))
     new_weights = call(
         functools.partial(apply_kernel, float(height * width * parts), 4),
         field,

time: 22.8 us -> 22.8 us (level)
  starting transfers between devices: 9.83 us -> 8.44 us
  waiting for transfers between devices: 5.23 us -> 6.61 us
    ppermute x2, starting transfers between devices: 1.66 us -> 0.26 us  [local(): lax.ppermute(squares, 'mp', [(at, at ^ flip) for at in range(parts)])]
    ppermute x2, waiting for transfers between devices: 1.64 us -> 3.02 us  [local(): lax.ppermute(squares, 'mp', [(at, at ^ flip) for at in range(parts)])]
where the time goes in v6:
time: 22.8 us; the launch traced here: 22.6 us
  starting transfers between devices  8.44 us (37%)
  Pallas kernels  6.82 us (30%)
  waiting for transfers between devices  6.61 us (29%)
  between operations  0.7 us (3%)
    ppermute x3, starting transfers between devices, local(): other = lax.ppermute(held, 'dp', [(at, at ^ bit) for at in range(replicas)])  8.17 us
    pallas_call x6, Pallas kernels, call(): pl.pallas_call(kernel, out_shape=shapes, in_specs=specs, out_specs=out_sp...  6.82 us
    ppermute x3, waiting for transfers between devices, local(): other = lax.ppermute(held, 'dp', [(at, at ^ bit) for at in range(replicas)])  3.59 us
    ppermute x2, waiting for transfers between devices, local(): lax.ppermute(squares, 'mp', [(at, at ^ flip) for at in range(parts)])  3.02 us
  transfers between devices with their start and end apart: 5, of which 5 were waited for; matrix products, arithmetic and copies ran while one was open for 0% of the time, Pallas kernels for 14%

profile of v6, /device:TPU:0, one launch (start us, length us, event | category | flops | bytes accessed | tf_op | source)
XLA Modules:
  0.0 22.6 jit_solution(1324932978287386049)
XLA Ops:
  0.6 1.8 %shard_map.77 = (f32[1,32,128]{2,1,0:T(8,128)S(1)}, f32[64,3584]{1,0:T(8,128)S(1)}, bf16[14,256,256]{2,1,0:T(8,128)(2,1)S(1)}, f32[14,64,128]{2,1,0:T(8,128)S(1)}) custom-call(bf16[1,64,3584]{2,1,0:T(8,128)(2,1)} %grad.1, f32[1,64,3584]{2,1,0:T(8,128)} %mom.1, s32[32,56]{1,0:T(8,128)} %bitcast.3, bf16[128,64]{1,0:T(8,128)(2,1)} %constant.4.clone.table), custom_call_target="tpu_custom_call" | custom-call | flops 1073741824 | bytes 1048576 | tf_op jit(solution)/shard_map/pallas_call | solution.py:248
  2.5 3.1 %collective-permute-start = (f32[1,32,128]{2,1,0:T(8,128)S(1)}, f32[1,32,128]{2,1,0:T(8,128)S(1)}, u32[]{:S(2)}, u32[]{:S(2)}) collective-permute-start(f32[1,32,128]{2,1,0:T(8,128)S(1)} %get-tuple-element.13.message), channel_id=1, source_target_pairs={{0,4},{4,0},{8,12},{12,8},{16,20},{20,16},{24,28},{28,24},{1,5},{5... | collective-permute-start | bytes 49160 | tf_op jit(solution)/shard_map/ppermute | solution.py:310
  5.5 1.5 %shard_map.78 = f32[1,64,3584]{2,1,0:T(8,128)} custom-call(f32[1,32,128]{2,1,0:T(8,128)S(1)} %get-tuple-element.13.message, f32[64,3584]{1,0:T(8,128)S(1)} %get-tuple-element.14.summed, bf16[14,256,256]{2,1,0:T(8,128)(2,1)S(1)} %get-tuple-element.15.sides, f32[14,64,128]{2,1,0:T(8,128)S(1)} %get-tuple-element.16.column), custom_call_target="tpu_custom_call" | custom-call | flops 2147483648 | bytes 1048576 | tf_op jit(solution)/shard_map/pallas_call | solution.py:248
  7.0 0.2 collective-permute-done
  7.2 2.1 %collective-permute-start.1 = (f32[2,32,128]{2,1,0:T(8,128)S(1)}, f32[2,32,128]{2,1,0:T(8,128)S(1)}, u32[]{:S(2)}, u32[]{:S(2)}) collective-permute-start(f32[2,32,128]{2,1,0:T(8,128)S(1)} %pad_maximum_fusion), channel_id=1, source_target_pairs={{0,8},{4,12},{8,0},{12,4},{16,24},{20,28},{24,16},{28,20},{1,9},{5... | collective-permute-start | bytes 98312 | tf_op jit(solution)/shard_map/ppermute | solution.py:310
  9.3 1.9 %collective-permute-done.1 = f32[2,32,128]{2,1,0:T(8,128)S(1)} collective-permute-done((f32[2,32,128]{2,1,0:T(8,128)S(1)}, f32[2,32,128]{2,1,0:T(8,128)S(1)}, u32[]{:S(2)}, u32[]{:S(2)}) %collective-permute-start.1) | collective-permute-done | bytes 32800 | tf_op jit(solution)/shard_map/ppermute | solution.py:310
  11.2 3.0 %collective-permute-start.2 = (f32[4,32,128]{2,1,0:T(8,128)S(1)}, f32[4,32,128]{2,1,0:T(8,128)S(1)}, u32[]{:S(2)}, u32[]{:S(2)}) collective-permute-start(f32[4,32,128]{2,1,0:T(8,128)S(1)} %constant_dynamic-update-slice_fusion.lists), channel_id=1, source_target_pairs={{0,16},{4,20},{8,24},{12,28},{16,0},{20,4},{24,8},{28,12},{1,17},{... | collective-permute-start | bytes 196616 | tf_op jit(solution)/shard_map/ppermute | solution.py:315
  14.3 0.7 %shard_map.79.held = f32[896,256]{1,0:T(8,128)S(1)} custom-call(f32[4,32,128]{2,1,0:T(8,128)S(1)} %constant_dynamic-update-slice_fusion.lists), custom_call_target="tpu_custom_call" | custom-call | flops 1073741824 | bytes 1048576 | tf_op jit(solution)/shard_map/pallas_call | solution.py:248
  15.0 0.0 copy-start.1
  15.0 1.5 %collective-permute-done.2.lists = f32[4,32,128]{2,1,0:T(8,128)S(1)} collective-permute-done((f32[4,32,128]{2,1,0:T(8,128)S(1)}, f32[4,32,128]{2,1,0:T(8,128)S(1)}, u32[]{:S(2)}, u32[]{:S(2)}) %collective-permute-start.2) | collective-permute-done | bytes 65568 | tf_op jit(solution)/shard_map/ppermute | solution.py:315
  16.5 0.7 %shard_map.80 = (f32[896,256]{1,0:T(8,128)S(1)}, f32[8,128]{1,0:T(8,128)S(1)}) custom-call(f32[4,32,128]{2,1,0:T(8,128)S(1)} %collective-permute-done.2.lists, f32[896,256]{1,0:T(8,128)S(1)} %shard_map.79.held), custom_call_target="tpu_custom_call" | custom-call | flops 1073741824 | bytes 1048576 | tf_op jit(solution)/shard_map/pallas_call | solution.py:248
  17.3 0.1 collective-permute-start.3
  17.3 0.0 copy-done.1
  17.3 0.0 copy-start
  17.4 0.9 %shard_map.81.update = f32[64,3584]{1,0:T(8,128)S(1)} custom-call(f32[896,256]{1,0:T(8,128)S(1)} %get-tuple-element.19.total, bf16[576,256]{1,0:T(8,128)(2,1)S(1)} %copy-done.1), custom_call_target="tpu_custom_call" | custom-call | flops 2147483648 | bytes 1048576 | tf_op jit(solution)/shard_map/pallas_call | solution.py:248
  18.3 2.0 %collective-permute-done.3 = f32[8,128]{1,0:T(8,128)S(1)} collective-permute-done((f32[8,128]{1,0:T(8,128)S(1)}, f32[8,128]{1,0:T(8,128)S(1)}, u32[]{:S(2)}, u32[]{:S(2)}) %collective-permute-start.3) | collective-permute-done | bytes 4128 | tf_op jit(solution)/shard_map/ppermute | solution.py:335
  20.4 0.2 collective-permute-start.4
  20.6 1.0 %collective-permute-done.4 = f32[8,128]{1,0:T(8,128)S(1)} collective-permute-done((f32[8,128]{1,0:T(8,128)S(1)}, f32[8,128]{1,0:T(8,128)S(1)}, u32[]{:S(2)}, u32[]{:S(2)}) %collective-permute-start.4) | collective-permute-done | bytes 4128 | tf_op jit(solution)/shard_map/ppermute | solution.py:335
  21.5 0.0 copy-done
  21.5 1.1 %shard_map.82 = f32[64,3584]{1,0:T(8,128)} custom-call(f32[64,3584]{1,0:T(8,128)S(1)} %copy-done, f32[64,3584]{1,0:T(8,128)S(1)} %shard_map.81.update, f32[8,128]{1,0:T(8,128)S(1)} %add.7.squares), custom_call_target="tpu_custom_call" | custom-call | flops 1048576 | bytes 1048576 | tf_op jit(solution)/shard_map/pallas_call | solution.py:248
  (5 shorter events, 0.0 us)
Async XLA Ops:
  2.5 4.8 %collective-permute-start = (f32[1,32,128]{2,1,0:T(8,128)S(1)}, f32[1,32,128]{2,1,0:T(8,128)S(1)}, u32[]{:S(2)}, u32[]{:S(2)}) collective-permute-start(f32[1,32,128]{2,1,0:T(8,128)S(1)} %get-tuple-element.13.message), channel_id=1, source_target_pairs={{0,4},{4,0},{8,12},{12,8},{16,20},{20,16},{24,28},{28,24},{1,5},{5... | collective-permute-start | bytes 49160 | tf_op jit(solution)/shard_map/ppermute | solution.py:310
  7.2 4.0 %collective-permute-start.1 = (f32[2,32,128]{2,1,0:T(8,128)S(1)}, f32[2,32,128]{2,1,0:T(8,128)S(1)}, u32[]{:S(2)}, u32[]{:S(2)}) collective-permute-start(f32[2,32,128]{2,1,0:T(8,128)S(1)} %pad_maximum_fusion), channel_id=1, source_target_pairs={{0,8},{4,12},{8,0},{12,4},{16,24},{20,28},{24,16},{28,20},{1,9},{5... | collective-permute-start | bytes 98312 | tf_op jit(solution)/shard_map/ppermute | solution.py:310
  11.2 5.3 %collective-permute-start.2 = (f32[4,32,128]{2,1,0:T(8,128)S(1)}, f32[4,32,128]{2,1,0:T(8,128)S(1)}, u32[]{:S(2)}, u32[]{:S(2)}) collective-permute-start(f32[4,32,128]{2,1,0:T(8,128)S(1)} %constant_dynamic-update-slice_fusion.lists), channel_id=1, source_target_pairs={{0,16},{4,20},{8,24},{12,28},{16,0},{20,4},{24,8},{28,12},{1,17},{... | collective-permute-start | bytes 196616 | tf_op jit(solution)/shard_map/ppermute | solution.py:315
  15.0 2.3 %copy-start.1 = (bf16[576,256]{1,0:T(8,128)(2,1)S(1)}, bf16[576,256]{1,0:T(8,128)(2,1)}, u32[]{:S(2)}) copy-start(bf16[576,256]{1,0:T(8,128)(2,1)} %constant.5.clone.tables) | copy-start | bytes 884740
  17.3 3.1 %collective-permute-start.3 = (f32[8,128]{1,0:T(8,128)S(1)}, f32[8,128]{1,0:T(8,128)S(1)}, u32[]{:S(2)}, u32[]{:S(2)}) collective-permute-start(f32[8,128]{1,0:T(8,128)S(1)} %get-tuple-element.18), channel_id=1, source_target_pairs={{0,3},{1,2},{2,1},{3,0},{4,7},{5,6},{6,5},{7,4},{8,11},{9,10},{10,... | collective-permute-start | bytes 12296 | tf_op jit(solution)/shard_map/ppermute | solution.py:335
  17.3 4.2 %copy-start = (f32[64,3584]{1,0:T(8,128)S(1)}, f32[64,3584]{1,0:T(8,128)}, u32[]{:S(2)}) copy-start(f32[64,3584]{1,0:T(8,128)} %weights.1) | copy-start | bytes 2752516
  20.4 1.2 %collective-permute-start.4 = (f32[8,128]{1,0:T(8,128)S(1)}, f32[8,128]{1,0:T(8,128)S(1)}, u32[]{:S(2)}, u32[]{:S(2)}) collective-permute-start(f32[8,128]{1,0:T(8,128)S(1)} %add.6), channel_id=1, source_target_pairs={{0,1},{1,0},{2,3},{3,2},{4,5},{5,4},{6,7},{7,6},{8,9},{9,8},{10,11... | collective-permute-start | bytes 12296 | tf_op jit(solution)/shard_map/ppermute | solution.py:335
